TPU v7x, 256 devices: a whole 4x4x8 slice. The times are simulated.
256 devices in a mesh: grp: 8 (over y, core), seq: 32 (over z, x).
Axes of the slice: x: 4, y: 4, z: 8, core: 2. Of those that a mesh axis runs over, the one named last changes fastest.
Arguments:
- points: bfloat16 [262144, 256], P(('grp', 'seq')), may hold values from -6 to 6
- hilbert_pos: int32 [2048], P(('grp', 'seq')), may hold values from 0 to 63, as said below
- valid_counts: int32 [2048], P(('grp', 'seq')), may hold values from 32 to 128
- norm_params: float32 [2, 4, 256], replicated, may hold values from 0.5 to 1.5
- qkv_weight: bfloat16 [2, 256, 768], replicated
- out_weight: bfloat16 [2, 256, 256], replicated, may hold values from -0.375 to 0.375
- up_weight: bfloat16 [2, 256, 1024], replicated, may hold values from -0.375 to 0.375
- down_weight: bfloat16 [2, 1024, 256], replicated, may hold values from -0.1875 to 0.1875
Outputs:
- features_out: bfloat16 [262144, 256], P(('grp', 'seq'))
Inputs may be any that keep to these rules, and one draw needn't show every extreme that they name: A group is the 8 devices with one index of seq. Within each group, hilbert_pos is a permutation of the group's 8 * 8 positions. The owner of position h is the device of index h // 8 along grp in the same group. Each device sends exactly 1 of its cells to each owner of its group.
All inputs are finite; a program needn't handle non-finite values.
Results may differ from a plain program's by a relative error of at most 0.017.
The roundings to bfloat16 on the way count: a program that leaves them out, or rounds other values in their place, can miss the bound.
Values may be sent and summed in bfloat16 or wider, within the bound.
A program may use at most 64 MiB of HBM per device.

v0:
```python
import math

import jax
import jax.numpy as jnp
from jax import lax
from jax.experimental import pallas as pl
from jax.experimental.pallas import tpu as pltpu
from jax.sharding import PartitionSpec as P

C = 256
HEADS = 16
HD = 16
HID = 1024
CELL = 128
CELLS = 8
ROWS = CELL * CELLS
HALF = ROWS // 2
STEP = 2 * CELL
F32 = jnp.float32
BF16 = jnp.bfloat16
I32 = jnp.int32
MESH = pl.DeviceIdType.MESH
SCORE_SCALE = HD**-0.5 * math.log2(math.e)
SAFE_EXPONENT = 60.0
SAFE_VALUE = 2.0**40


def nt_dot(a, b):
    return lax.dot_general(a, b, (((1,), (1,)), ((), ())), preferred_element_type=F32)


def nn_dot(a, b):
    return jnp.dot(a, b, preferred_element_type=F32)


def norm_rows_of(values, gain, offset):
    center = jnp.mean(values, axis=-1, keepdims=True)
    spread = values - center
    second = jnp.mean(spread * spread, axis=-1, keepdims=True)
    return spread * lax.rsqrt(second + 1e-5) * gain + offset


def head_pick(rows, columns, channel_axis):
    channel = lax.broadcasted_iota(I32, (rows, columns), channel_axis) // HD
    head = lax.broadcasted_iota(I32, (rows, columns), 1 - channel_axis)
    return jnp.where(channel == head, 1.0, 0.0).astype(BF16)


def first_valid(rows, count):
    index = lax.broadcasted_iota(I32, (CELL, 1), 0)
    return jnp.where(index < count, rows, rows[0:1, :])


def lane_valid(count):
    return jnp.where(lax.broadcasted_iota(I32, (1, CELL), 1) < count, 1.0, 0.0)


def project(rows, valid, gain, offset, w_t, w_k, k_ref, v_ref, q_ref, peak_ref, k_at, q_at):
    count = rows.shape[0]
    normed = norm_rows_of(rows, gain, offset).astype(BF16)
    keys = nn_dot(normed, w_k).astype(BF16)
    k_ref[pl.ds(k_at, count), :] = keys
    values = nt_dot(w_t[C:, :], normed) * valid
    v_ref[:, pl.ds(k_at, count)] = values.astype(BF16)
    wide = keys.astype(F32)
    sums = nn_dot((wide * wide).astype(BF16), head_pick(C, CELL, 0))
    peak_ref[0:1, :] = jnp.maximum(peak_ref[0:1, :], jnp.max(sums, axis=0, keepdims=True))
    tall = jnp.max(jnp.abs(values), axis=0, keepdims=True)
    peak_ref[2:3, :] = jnp.maximum(peak_ref[2:3, :], jnp.maximum(tall[:, :CELL], tall[:, count - CELL :]))
    if q_at is not None:
        queries = nt_dot(w_t[:C, :], normed).astype(BF16)
        q_ref[:, pl.ds(q_at, count)] = queries
        wide = queries.astype(F32)
        sums = nn_dot(head_pick(HEADS, C, 1), (wide * wide).astype(BF16))
        tall = jnp.max(sums, axis=0, keepdims=True)
        peak_ref[1:2, :] = jnp.maximum(peak_ref[1:2, :], jnp.maximum(tall[:, :CELL], tall[:, count - CELL :]))


def turn(qkv_ref, w_ref):
    for at, source in ((0, 0), (C, 2 * C)):
        w_ref[at : at + C, :] = qkv_ref[:, source : source + C].astype(F32).T.astype(BF16)


def attend(windows, pads, k_ref, v_ref, q_ref, m_ref, exact, unroll):
    def one_head(head):
        row = pl.multiple_of(head * HD, HD)
        half = pl.ds(pl.multiple_of((head // 8) * CELL, CELL), CELL)
        for q_lo, q_n, k_lo, k_n in windows:
            lane_head = lax.broadcasted_iota(I32, (CELL, q_n), 0) // HD
            queries = q_ref[half, q_lo : q_lo + q_n]
            queries = jnp.where(lane_head == head % 8, queries, jnp.zeros_like(queries))
            scores = nn_dot(k_ref[k_lo : k_lo + k_n, half], queries)
            if exact:
                scores = scores - jnp.max(scores, axis=0, keepdims=True)
            weights = jnp.exp2(scores * SCORE_SCALE)
            total = jnp.sum(jnp.sum(weights.reshape(k_n // 8, 8, q_n), axis=0), axis=0, keepdims=True)
            for cell in range(k_n // CELL):
                total = total - pads[k_lo // CELL + cell] * weights[cell * CELL : cell * CELL + 1, :]
            mixed = nn_dot(v_ref[pl.ds(row, HD), k_lo : k_lo + k_n], weights.astype(BF16))
            m_ref[pl.ds(row, HD), q_lo : q_lo + q_n] = (mixed / total).astype(BF16)

    def step(i, carry):
        for u in range(unroll):
            one_head(i * unroll + u)
        return carry

    lax.fori_loop(0, HEADS // unroll, step, 0)


def attend_any(windows, pads, peak_ref, k_ref, v_ref, q_ref, m_ref):
    bound = peak_ref[0, 0] * peak_ref[1, 0] * SCORE_SCALE**2
    safe = (bound < SAFE_EXPONENT * SAFE_EXPONENT) & (peak_ref[2, 0] < SAFE_VALUE)

    @pl.when(safe)
    def _():
        attend(windows, pads, k_ref, v_ref, q_ref, m_ref, False, 4)

    @pl.when(jnp.logical_not(safe))
    def _():
        attend(windows, pads, k_ref, v_ref, q_ref, m_ref, True, 1)


def gelu(values):
    return 0.5 * values * (1.0 + lax.erf(values * (2.0**-0.5)))


def finish(rows, mixture_t, gain, offset, out_w, up_w, down_w):
    residual = rows.astype(F32) + nn_dot(mixture_t.astype(F32).T.astype(BF16), out_w)
    residual = residual.astype(BF16).astype(F32)
    normed = norm_rows_of(residual, gain, offset).astype(BF16)
    hidden = gelu(nn_dot(normed, up_w)).astype(BF16)
    return (residual + nn_dot(hidden, down_w)).astype(BF16)


def widest(peak_ref):
    peak_ref[...] = jnp.broadcast_to(jnp.max(peak_ref[...], axis=1, keepdims=True), peak_ref.shape)


def started(*pairs):
    copies = [pltpu.make_async_copy(*pair) for pair in pairs]
    for copy in copies:
        copy.start()
    return copies


def finished(copies):
    for copy in copies:
        copy.wait()


def gather_kernel(
    pos_ref, count_ref, x_hbm, norm_ref, qkv_hbm,
    cells_hbm, k_hbm, v_hbm, q_hbm, meta_ref, peak_ref,
    x_buf, out_buf, in_buf, note_out, note_in, qkv_ref, w_ref, k_ref, v_ref, q_ref,
    load_sem, store_sem, send, recv, note_send, note_recv,
):
    me, seq = lax.axis_index("grp"), lax.axis_index("seq")
    barrier = pltpu.get_barrier_semaphore()
    for r in range(1, CELLS):
        pl.semaphore_signal(barrier, inc=1, device_id=(lax.rem(me + r, CELLS), seq), device_id_type=MESH)
    loads = started((x_hbm, x_buf, load_sem.at[0]), (qkv_hbm.at[0], qkv_ref, load_sem.at[1]))
    finished(loads[:1])
    row = lax.broadcasted_iota(I32, (CELLS, CELL), 0)
    for owner in range(CELLS):
        index, place, count = jnp.int32(0), jnp.int32(0), jnp.int32(0)
        for j in range(CELLS):
            position = pos_ref[j]
            mine = position // CELLS == owner
            index = jnp.where(mine, j, index)
            place = jnp.where(mine, position % CELLS, place)
            count = jnp.where(mine, count_ref[j], count)
        out_buf[owner] = x_buf[index]
        note_out[owner] = jnp.where(row == 0, place, count)
    finished(loads[1:])
    turn(qkv_ref, w_ref)
    pl.semaphore_wait(barrier, CELLS - 1)

    def sent(r):
        owner = lax.rem(me + r, CELLS)
        return (
            pltpu.make_async_remote_copy(
                out_buf.at[owner], in_buf.at[me], send.at[r], recv.at[r],
                device_id=(owner, seq), device_id_type=MESH),
            pltpu.make_async_remote_copy(
                note_out.at[owner], note_in.at[me], note_send.at[r], note_recv.at[r],
                device_id=(owner, seq), device_id_type=MESH),
        )

    copies = [sent(r) for r in range(1, CELLS)]
    for pair in copies:
        for copy in pair:
            copy.start()
    gain, offset = norm_ref[0, 0:1, :], norm_ref[0, 1:2, :]
    peak_ref[...] = jnp.zeros_like(peak_ref)

    def take(j):
        at = pl.multiple_of(j * CELL, CELL)
        count = note_in[j, 1:2, :]
        rows = first_valid(in_buf[j].astype(F32), count[:, 0:1])
        project(
            rows, lane_valid(count), gain, offset, w_ref[...], qkv_ref[:, C : 2 * C],
            k_ref, v_ref, q_ref, peak_ref, at, at,
        )

    def given(r):
        j = lax.rem(me - r + CELLS, CELLS)
        lanes = pl.ds(pl.multiple_of(j * CELL, CELL), CELL)
        return (
            (in_buf.at[j], cells_hbm.at[j], store_sem.at[r, 0]),
            (k_ref.at[lanes, :], k_hbm.at[lanes, :], store_sem.at[r, 1]),
            (v_ref.at[:, lanes], v_hbm.at[:, lanes], store_sem.at[r, 2]),
            (q_ref.at[:, lanes], q_hbm.at[:, lanes], store_sem.at[r, 3]),
        )

    in_buf[me] = out_buf[me]
    note_in[me] = note_out[me]
    take(me)
    started(*given(0))

    def arrive(r, carry):
        for copy in sent(r):
            copy.wait_recv()
        take(lax.rem(me - r + CELLS, CELLS))
        started(*given(r))
        return carry

    lax.fori_loop(1, CELLS, arrive, 0)
    lane = lax.broadcasted_iota(I32, (CELLS, CELL), 1)
    meta = jnp.zeros((CELLS, CELL), I32)
    for j in range(CELLS):
        meta = jnp.where(lane == j, note_in[j], meta)
    meta_ref[...] = meta
    widest(peak_ref)
    for pair in copies:
        for copy in pair:
            copy.wait_send()
    for r in range(CELLS):
        finished([pltpu.make_async_copy(*triple) for triple in given(r)])


def vmem():
    return pl.BlockSpec(memory_space=pltpu.VMEM)


def smem():
    return pl.BlockSpec(memory_space=pltpu.SMEM)


def hbm():
    return pl.BlockSpec(memory_space=pl.ANY)


def shape(dims, dtype=BF16):
    return jax.ShapeDtypeStruct(dims, dtype)


def dma(*dims):
    return pltpu.SemaphoreType.DMA(dims)


def gather_cells(pos, counts, cells, norms, qkv):
    return pl.pallas_call(
        gather_kernel,
        out_shape=(
            shape((CELLS, CELL, C)), shape((ROWS, C)), shape((C, ROWS)), shape((C, ROWS)),
            shape((CELLS, CELL), I32), shape((CELLS, CELL), F32),
        ),
        in_specs=[smem(), smem(), hbm(), vmem(), hbm()],
        out_specs=(hbm(), hbm(), hbm(), hbm(), vmem(), vmem()),
        scratch_shapes=[
            pltpu.VMEM((CELLS, CELL, C), BF16),
            pltpu.VMEM((CELLS, CELL, C), BF16),
            pltpu.VMEM((CELLS, CELL, C), BF16),
            pltpu.VMEM((CELLS, CELLS, CELL), I32),
            pltpu.VMEM((CELLS, CELLS, CELL), I32),
            pltpu.VMEM((C, 3 * C), BF16),
            pltpu.VMEM((2 * C, C), BF16),
            pltpu.VMEM((ROWS, C), BF16),
            pltpu.VMEM((C, ROWS), BF16),
            pltpu.VMEM((C, ROWS), BF16),
            dma(2), dma(CELLS, 4), dma(CELLS), dma(CELLS), dma(CELLS), dma(CELLS),
        ],
        compiler_params=pltpu.CompilerParams(
            collective_id=0, has_side_effects=True, vmem_limit_bytes=24 * 2**20),
        name="gather_cells",
    )(pos, counts, cells, norms, qkv)


def aligned_kernel(
    meta_hbm, peak_hbm, k_hbm, v_hbm, q_hbm, cells_hbm, m_ref, placed_hbm, count_ref,
    meta_ref, peak_ref, k_ref, v_ref, q_ref, sems, place_sems,
):
    loads = started(
        (meta_hbm, meta_ref, sems.at[0]), (peak_hbm, peak_ref, sems.at[1]),
        (k_hbm, k_ref, sems.at[2]), (v_hbm, v_ref, sems.at[3]),
    )
    finished(loads[:1])
    moves, places = [], []
    for j in range(CELLS):
        to = meta_ref[0, j]
        lanes = pl.ds(pl.multiple_of(to * CELL, CELL), CELL)
        moves += started((q_hbm.at[:, pl.ds(j * CELL, CELL)], q_ref.at[:, lanes], place_sems.at[0, j]))
        places += started((cells_hbm.at[j], placed_hbm.at[to], place_sems.at[1, j]))
        count_ref[pl.ds(to, 1), :] = jnp.full((1, CELL), meta_ref[1, j], I32)
    finished(loads[1:])
    finished(moves)
    pads = [(CELL - meta_ref[1, j]).astype(F32) for j in range(CELLS)]
    attend_any(((0, HALF, 0, ROWS), (HALF, HALF, 0, ROWS)), pads, peak_ref, k_ref, v_ref, q_ref, m_ref)
    finished(places)


def aligned_attention(meta, peak, keys, values, queries, cells):
    return pl.pallas_call(
        aligned_kernel,
        out_shape=(shape((C, ROWS)), shape((CELLS, CELL, C)), shape((CELLS, CELL), I32)),
        in_specs=[hbm()] * 6,
        out_specs=(vmem(), hbm(), vmem()),
        scratch_shapes=[
            pltpu.SMEM((CELLS, CELL), I32),
            pltpu.SMEM((CELLS, CELL), F32),
            pltpu.VMEM((ROWS, C), BF16),
            pltpu.VMEM((C, ROWS), BF16),
            pltpu.VMEM((C, ROWS), BF16),
            dma(4), dma(2, CELLS),
        ],
        compiler_params=pltpu.CompilerParams(vmem_limit_bytes=48 * 2**20),
        name="aligned_attention",
    )(meta, peak, keys, values, queries, cells)


def along(step):
    n_grp, n_seq = lax.axis_size("grp"), lax.axis_size("seq")
    flat = lax.axis_index("grp") * n_seq + lax.axis_index("seq")
    other = lax.rem(flat + step + n_grp * n_seq, n_grp * n_seq)
    return (other // n_seq, lax.rem(other, n_seq))


def middle_kernel(
    note_ref, x_hbm, m_hbm, norm_ref, qkv_hbm, out_hbm, up_hbm, down_hbm,
    y_hbm, k_hbm, v_hbm, q_hbm, all_count_ref, peak_ref,
    x_ref, m_ref, qkv_ref, out_ref, up_ref, down_ref,
    y_ref, before_ref, after_ref, note_before, note_after, w_ref, k_ref, v_ref, q_ref,
    load_sem, store_sem, send_before, send_after, recv_before, recv_after, note_send, note_recv,
):
    after, before = along(1), along(-1)
    barrier = pltpu.get_barrier_semaphore()
    for device in (after, before):
        pl.semaphore_signal(barrier, inc=1, device_id=device, device_id_type=MESH)
    loads = started(
        (x_hbm, x_ref, load_sem.at[0]),
        (m_hbm, m_ref, load_sem.at[1]),
        (out_hbm.at[0], out_ref, load_sem.at[2]),
        (up_hbm.at[0], up_ref, load_sem.at[3]),
        (down_hbm.at[0], down_ref, load_sem.at[4]),
        (qkv_hbm.at[1], qkv_ref, load_sem.at[5]),
    )
    finished(loads[5:])
    turn(qkv_ref, w_ref)
    finished(loads[:5])
    pl.semaphore_wait(barrier, 2)
    notes = [
        pltpu.make_async_remote_copy(
            note_ref, target, note_send.at[i], note_recv.at[i], device_id=device, device_id_type=MESH)
        for i, (target, device) in enumerate(((note_after, before), (note_before, after)))
    ]
    for copy in notes:
        copy.start()
    gain, offset = norm_ref[1, 0:1, :], norm_ref[1, 1:2, :]
    peak_ref[...] = jnp.zeros_like(peak_ref)

    def to_before(i):
        return pltpu.make_async_remote_copy(
            y_ref.at[pl.ds(i * STEP, STEP)], after_ref.at[pl.ds(i * STEP, STEP)],
            send_before.at[i], recv_after.at[i], device_id=before, device_id_type=MESH)

    def to_after(i):
        return pltpu.make_async_remote_copy(
            y_ref.at[pl.ds(HALF + i * STEP, STEP)], before_ref.at[pl.ds(i * STEP, STEP)],
            send_after.at[i], recv_before.at[i], device_id=after, device_id_type=MESH)

    def place(rows, pair, k_at, q_at):
        wide = rows.astype(F32)
        wide = jnp.concatenate(
            [first_valid(wide[u * CELL : (u + 1) * CELL], pair[u]) for u in range(2)], axis=0)
        valid = jnp.concatenate([lane_valid(pair[u]) for u in range(2)], axis=1)
        project(
            wide, valid, gain, offset, w_ref[...], qkv_ref[:, C : 2 * C],
            k_ref, v_ref, q_ref, peak_ref, k_at, q_at,
        )

    for i in range(2):
        for chunk, copy in ((i, to_before(i)), (2 + i, to_after(i))):
            at = chunk * STEP
            cells = (2 * chunk, 2 * chunk + 1)
            rows = jnp.concatenate([x_ref[p] for p in cells], axis=0)
            mixture = m_ref[:, at : at + STEP]
            done = finish(
                rows, mixture, norm_ref[0, 2:3, :], norm_ref[0, 3:4, :],
                out_ref[...], up_ref[...], down_ref[...],
            )
            y_ref[at : at + STEP, :] = done
            place(done, [note_ref[p : p + 1, 0:1] for p in cells], HALF + at, at)
            copy.start()
    own = pl.ds(HALF, ROWS)
    stores = started(
        (y_ref, y_hbm, store_sem.at[0]),
        (k_ref.at[own, :], k_hbm.at[own, :], store_sem.at[1]),
        (v_ref.at[:, own], v_hbm.at[:, own], store_sem.at[2]),
        (q_ref, q_hbm, store_sem.at[3]),
    )
    for copy in notes:
        copy.wait()
    for i in range(2):
        for incoming, source, note, first, k_first, at_sem in (
            (to_before(i), after_ref, note_after, 2 * i, HALF + ROWS, 4),
            (to_after(i), before_ref, note_before, CELLS // 2 + 2 * i, 0, 8),
        ):
            incoming.wait_recv()
            pair = [note[first + u : first + u + 1, 0:1] for u in range(2)]
            k_at = k_first + i * STEP
            place(source[i * STEP : (i + 1) * STEP, :], pair, k_at, None)
            part = pl.ds(k_at, STEP)
            stores += started(
                (k_ref.at[part, :], k_hbm.at[part, :], store_sem.at[at_sem + 2 * i]),
                (v_ref.at[:, part], v_hbm.at[:, part], store_sem.at[at_sem + 2 * i + 1]),
            )
    all_count_ref[0:4, :] = note_before[4:8, :]
    all_count_ref[4:12, :] = note_ref[...]
    all_count_ref[12:16, :] = note_after[0:4, :]
    widest(peak_ref)
    for i in range(2):
        to_before(i).wait_send()
        to_after(i).wait_send()
    finished(stores)


def middle(notes, cells, mixture, norms, qkv, out_w, up_w, down_w):
    return pl.pallas_call(
        middle_kernel,
        out_shape=(
            shape((ROWS, C)), shape((2 * ROWS, C)), shape((C, 2 * ROWS)), shape((C, ROWS)),
            shape((2 * CELLS, CELL), I32), shape((CELLS, CELL), F32),
        ),
        in_specs=[vmem()] + [hbm()] * 2 + [vmem()] + [hbm()] * 4,
        out_specs=(hbm(),) * 4 + (vmem(), vmem()),
        scratch_shapes=[
            pltpu.VMEM((CELLS, CELL, C), BF16),
            pltpu.VMEM((C, ROWS), BF16),
            pltpu.VMEM((C, 3 * C), BF16),
            pltpu.VMEM((C, C), BF16),
            pltpu.VMEM((C, HID), BF16),
            pltpu.VMEM((HID, C), BF16),
            pltpu.VMEM((ROWS, C), BF16),
            pltpu.VMEM((HALF, C), BF16),
            pltpu.VMEM((HALF, C), BF16),
            pltpu.VMEM((CELLS, CELL), I32),
            pltpu.VMEM((CELLS, CELL), I32),
            pltpu.VMEM((2 * C, C), BF16),
            pltpu.VMEM((2 * ROWS, C), BF16),
            pltpu.VMEM((C, 2 * ROWS), BF16),
            pltpu.VMEM((C, ROWS), BF16),
            dma(6), dma(12), dma(2), dma(2), dma(2), dma(2), dma(2), dma(2),
        ],
        compiler_params=pltpu.CompilerParams(
            collective_id=1, has_side_effects=True, vmem_limit_bytes=40 * 2**20),
        name="middle",
    )(notes, cells, mixture, norms, qkv, out_w, up_w, down_w)


def shifted_kernel(
    count_hbm, peak_hbm, k_hbm, v_hbm, q_hbm, x_hbm, norm_ref, out_hbm, up_hbm, down_hbm,
    y_hbm,
    count_ref, peak_ref, k_ref, v_ref, q_ref, x_ref, out_ref, up_ref, down_ref, m_ref, y_ref,
    load_sem, store_sem,
):
    loads = started(
        (k_hbm, k_ref, load_sem.at[0]), (q_hbm, q_ref, load_sem.at[1]), (v_hbm, v_ref, load_sem.at[2]),
        (count_hbm, count_ref, load_sem.at[3]), (peak_hbm, peak_ref, load_sem.at[4]),
        (x_hbm, x_ref, load_sem.at[5]), (out_hbm.at[1], out_ref, load_sem.at[6]),
        (up_hbm.at[1], up_ref, load_sem.at[7]), (down_hbm.at[1], down_ref, load_sem.at[8]),
    )
    finished(loads[:5])
    pads = [(CELL - count_ref[j, 0]).astype(F32) for j in range(2 * CELLS)]
    attend_any(((0, HALF, 0, ROWS), (HALF, HALF, ROWS, ROWS)), pads, peak_ref, k_ref, v_ref, q_ref, m_ref)
    finished(loads[5:])
    stores = []
    for i in range(ROWS // STEP):
        at = i * STEP
        done = finish(
            x_ref[at : at + STEP, :], m_ref[:, at : at + STEP], norm_ref[1, 2:3, :], norm_ref[1, 3:4, :],
            out_ref[...], up_ref[...], down_ref[...],
        )
        for u in range(2):
            index = lax.broadcasted_iota(I32, (CELL, 1), 0)
            keep = index < count_ref[CELLS // 2 + 2 * i + u, 0]
            part = done[u * CELL : (u + 1) * CELL, :]
            y_ref[at + u * CELL : at + (u + 1) * CELL, :] = jnp.where(keep, part, jnp.zeros_like(part))
        rows = pl.ds(at, STEP)
        stores += started((y_ref.at[rows], y_hbm.at[rows], store_sem.at[i]))
    finished(stores)


def shifted_block(counts, peak, keys, values, queries, rows, norms, out_w, up_w, down_w):
    return pl.pallas_call(
        shifted_kernel,
        out_shape=shape((ROWS, C)),
        in_specs=[hbm()] * 6 + [vmem()] + [hbm()] * 3,
        out_specs=hbm(),
        scratch_shapes=[
            pltpu.SMEM((2 * CELLS, CELL), I32),
            pltpu.SMEM((CELLS, CELL), F32),
            pltpu.VMEM((2 * ROWS, C), BF16),
            pltpu.VMEM((C, 2 * ROWS), BF16),
            pltpu.VMEM((C, ROWS), BF16),
            pltpu.VMEM((ROWS, C), BF16),
            pltpu.VMEM((C, C), BF16),
            pltpu.VMEM((C, HID), BF16),
            pltpu.VMEM((HID, C), BF16),
            pltpu.VMEM((C, ROWS), BF16),
            pltpu.VMEM((ROWS, C), BF16),
            dma(9), dma(4),
        ],
        compiler_params=pltpu.CompilerParams(vmem_limit_bytes=48 * 2**20),
        name="shifted_block",
    )(counts, peak, keys, values, queries, rows, norms, out_w, up_w, down_w)


def body(points, hilbert_pos, valid_counts, norms, qkv, out_w, up_w, down_w):
    cells, keys, values, queries, meta, peak = gather_cells(
        hilbert_pos, valid_counts, points.reshape(CELLS, CELL, C), norms, qkv)
    mixture, placed, notes = aligned_attention(meta, peak, keys, values, queries, cells)
    rows, keys, values, queries, counts, peak = middle(notes, placed, mixture, norms, qkv, out_w, up_w, down_w)
    return shifted_block(counts, peak, keys, values, queries, rows, norms, out_w, up_w, down_w)


def solution(mesh):
    return jax.shard_map(
        body,
        mesh=mesh,
        in_specs=(
            P(("grp", "seq"), None), P(("grp", "seq")), P(("grp", "seq")), P(), P(), P(), P(), P(),
        ),
        out_specs=P(("grp", "seq"), None),
        check_vma=False,
    )
```

profile of v0, /device:TPU:1, one launch (start us, length us, event | category | flops | bytes accessed | tf_op | source)
XLA Modules:
  0.0 99.4 jit_solution(15269829697499629203)
XLA Ops:
  0.0 0.0 copy-start.9
  0.0 0.0 copy-start.8
  0.0 0.7 copy-done.9
  0.7 0.0 copy-done.8
  0.7 0.0 copy-start.2
  0.7 1.1 %copy-done.2 = bf16[2,256,768]{2,1,0:T(8,128)(2,1)S(1)} copy-done((bf16[2,256,768]{2,1,0:T(8,128)(2,1)S(1)}, bf16[2,256,768]{2,1,0:T(8,128)(2,1)}, u32[]{:S(2)}) %copy-start.2) | copy-done | bytes 786456
  1.8 0.0 copy-start.5
  1.8 1.0 %copy-done.5 = bf16[1024,256]{1,0:T(8,128)(2,1)S(1)} copy-done((bf16[1024,256]{1,0:T(8,128)(2,1)S(1)}, bf16[1024,256]{1,0:T(8,128)(2,1)}, u32[]{:S(2)}) %copy-start.5) | copy-done | bytes 524312
  2.8 0.0 copy-start.6
  2.9 0.7 copy-done.6
  3.5 0.0 copy-start.3
  3.5 0.0 copy-start.4
  3.5 17.4 %gather_cells.1 = (bf16[8,128,256]{2,1,0:T(8,128)(2,1)S(1)}, bf16[1024,256]{1,0:T(8,128)(2,1)S(1)}, bf16[256,1024]{1,0:T(8,128)(2,1)S(1)}, bf16[256,1024]{1,0:T(...) custom-call(s32[8]{0:T(128)S(1)} %copy-done.8, s32[8]{0:T(128)S(1)} %copy-done.9, ...), custom_call_target="tpu_custom_call" | custom-call | tf_op jit(solution)/shard_map/gather_cells/pallas_call | solution.py:262
  21.0 0.0 copy-start
  21.0 0.0 copy-start.1
  21.0 0.0 copy-start.7
  21.0 28.1 %aligned_attention.1 = (bf16[256,1024]{1,0:T(8,128)(2,1)S(1)}, bf16[8,128,256]{2,1,0:T(8,128)(2,1)S(1)}, s32[8,128]{1,0:T(8,128)S(1)}) custom-call(s32[8,128]{1,0:T(8,128)S(1)} %get-tuple-element.20.meta_hbm, f32[8,128]{1,0:T(8,128)S(1)} %get-tuple-element.21.peak_hbm, bf16[1024,256]{1,0:T(8,128)(2,1)S(1)} %get-tuple-element.22.k_hbm, ...), custom_call_target="tpu_custom_call" | custom-call | tf_op jit(solution)/shard_map/aligned_attention/pallas_call | solution.py:313
  49.1 0.0 copy-done.3
  49.1 0.0 copy-done.4
  49.1 0.0 copy-done
  49.2 0.0 copy-done.1
  49.2 0.0 copy-done.7
  49.2 19.4 %middle.1 = (bf16[1024,256]{1,0:T(8,128)(2,1)S(1)}, bf16[2048,256]{1,0:T(8,128)(2,1)S(1)}, bf16[256,2048]{1,0:T(8,128)(2,1)S(1)}, bf16[256,1024]{1,0:T(8,128)(2,...) custom-call(s32[8,128]{1,0:T(8,128)S(1)} %get-tuple-element.26.note_ref, ...), custom_call_target="tpu_custom_call" | custom-call | tf_op jit(solution)/shard_map/middle/pallas_call | solution.py:438
  68.6 30.6 %shifted_block.1 = bf16[1024,256]{1,0:T(8,128)(2,1)} custom-call(s32[16,128]{1,0:T(8,128)S(1)} %get-tuple-element.29.count_hbm, f32[8,128]{1,0:T(8,128)S(1)} %get-tuple-element.30.peak_hbm, bf16[2048,256]{1,0:T(8,128)(2,1)S(1)} %get-tuple-element.31.k_hbm, bf16[256,2048]{1,0:T(8,128)(2,1)S(1)} %get-tuple-element.32.v_hbm, ...), custom_call_target="tpu_custom_call" | custom-call | tf_op jit(solution)/shard_map/shifted_block/pallas_call | solution.py:504
Async XLA Ops:
  0.0 0.7 copy-start.9
  0.0 0.7 copy-start.8
  0.7 1.1 %copy-start.2 = (bf16[2,256,768]{2,1,0:T(8,128)(2,1)S(1)}, bf16[2,256,768]{2,1,0:T(8,128)(2,1)}, u32[]{:S(2)}) copy-start(bf16[2,256,768]{2,1,0:T(8,128)(2,1)} %qkv_hbm.3) | copy-start | bytes 2359300
  1.8 1.0 %copy-start.5 = (bf16[1024,256]{1,0:T(8,128)(2,1)S(1)}, bf16[1024,256]{1,0:T(8,128)(2,1)}, u32[]{:S(2)}) copy-start(bf16[1024,256]{1,0:T(8,128)(2,1)} %param.8) | copy-start | bytes 1572868
  2.8 0.7 copy-start.6
  3.5 45.6 %copy-start.3 = (bf16[2,256,768]{2,1,0:T(8,128)(2,1)S(1)}, bf16[2,256,768]{2,1,0:T(8,128)(2,1)}, u32[]{:S(2)}) copy-start(bf16[2,256,768]{2,1,0:T(8,128)(2,1)} %qkv_hbm.3) | copy-start | bytes 2359300
  3.5 45.6 %copy-start.4 = (bf16[2,256,256]{2,1,0:T(8,128)(2,1)S(1)}, bf16[2,256,256]{2,1,0:T(8,128)(2,1)}, u32[]{:S(2)}) copy-start(bf16[2,256,256]{2,1,0:T(8,128)(2,1)} %out_hbm.3) | copy-start | bytes 786436
  21.0 28.2 %copy-start = (bf16[2,256,1024]{2,1,0:T(8,128)(2,1)S(1)}, bf16[2,256,1024]{2,1,0:T(8,128)(2,1)}, u32[]{:S(2)}) copy-start(bf16[2,256,1024]{2,1,0:T(8,128)(2,1)} %up_hbm.3) | copy-start | bytes 3145732
  21.0 28.2 %copy-start.1 = (bf16[2,1024,256]{2,1,0:T(8,128)(2,1)S(1)}, bf16[2,1024,256]{2,1,0:T(8,128)(2,1)}, u32[]{:S(2)}) copy-start(bf16[2,1024,256]{2,1,0:T(8,128)(2,1)} %down_hbm.3) | copy-start | bytes 3145732
  21.0 28.2 %copy-start.7 = (f32[2,4,256]{2,1,0:T(4,128)S(1)}, f32[2,4,256]{2,1,0:T(4,128)}, u32[]{:S(2)}) copy-start(f32[2,4,256]{2,1,0:T(4,128)} %norm_ref.5) | copy-start | bytes 24580
where the time goes:
time: 99.6 us; the launch traced here: 99.4 us
  Pallas kernels  95.6 us (96%)
  local copies, waits for them, and re-layouts  3.57 us (4%)
    pallas_call x1, Pallas kernels, shifted_block(): pl.pallas_call(shifted_kernel, out_shape=shape((ROWS, C)), in_specs=[hbm(...  30.6 us
    pallas_call x1, Pallas kernels, aligned_attention(): pl.pallas_call(aligned_kernel, out_shape=(shape((C, ROWS)), shape((CELLS,...  28.1 us
    pallas_call x1, Pallas kernels, middle(): pl.pallas_call(middle_kernel, out_shape=(shape((ROWS, C)), shape((2 * ROW...  19.4 us
    pallas_call x1, Pallas kernels, gather_cells(): pl.pallas_call(gather_kernel, out_shape=(shape((CELLS, CELL, C)), shape((...  17.4 us
    unnamed x20, local copies, waits for them, and re-layouts  3.57 us

commit v1 on v0

v1 whole, which is shorter than its diff:
```python
import math

import jax
import jax.numpy as jnp
from jax import lax
from jax.experimental import pallas as pl
from jax.experimental.pallas import tpu as pltpu
from jax.sharding import PartitionSpec as P

C = 256
HEADS = 16
HD = 16
HID = 1024
CELL = 128
CELLS = 8
ROWS = CELL * CELLS
HALF = ROWS // 2
STEP = 2 * CELL
F32 = jnp.float32
BF16 = jnp.bfloat16
I32 = jnp.int32
MESH = pl.DeviceIdType.MESH
SCORE_SCALE = HD**-0.5 * math.log2(math.e)
SAFE_EXPONENT = 60.0
SAFE_VALUE = 2.0**40


def nt_dot(a, b):
    return lax.dot_general(a, b, (((1,), (1,)), ((), ())), preferred_element_type=F32)


def nn_dot(a, b):
    return jnp.dot(a, b, preferred_element_type=F32)


def norm_rows_of(values, gain, offset):
    center = jnp.mean(values, axis=-1, keepdims=True)
    spread = values - center
    second = jnp.mean(spread * spread, axis=-1, keepdims=True)
    return spread * lax.rsqrt(second + 1e-5) * gain + offset


def head_pick(rows, columns, channel_axis):
    channel = lax.broadcasted_iota(I32, (rows, columns), channel_axis) // HD
    head = lax.broadcasted_iota(I32, (rows, columns), 1 - channel_axis)
    return jnp.where(channel == head, 1.0, 0.0).astype(BF16)


def first_valid(rows, count):
    index = lax.broadcasted_iota(I32, (CELL, 1), 0)
    return jnp.where(index < count, rows, rows[0:1, :])


def lane_valid(count):
    return jnp.where(lax.broadcasted_iota(I32, (1, CELL), 1) < count, 1.0, 0.0)


def project(rows, valid, gain, offset, w_t, w_k, k_ref, v_ref, q_ref, peak_ref, k_at, q_at):
    count = rows.shape[0]
    normed = norm_rows_of(rows, gain, offset).astype(BF16)
    keys = nn_dot(normed, w_k).astype(BF16)
    k_ref[pl.ds(k_at, count), :] = keys
    values = nt_dot(w_t[C:, :], normed) * valid
    v_ref[:, pl.ds(k_at, count)] = values.astype(BF16)
    wide = keys.astype(F32)
    sums = nn_dot((wide * wide).astype(BF16), head_pick(C, CELL, 0))
    peak_ref[0:1, :] = jnp.maximum(peak_ref[0:1, :], jnp.max(sums, axis=0, keepdims=True))
    tall = jnp.max(jnp.abs(values), axis=0, keepdims=True)
    peak_ref[2:3, :] = jnp.maximum(peak_ref[2:3, :], jnp.maximum(tall[:, :CELL], tall[:, count - CELL :]))
    if q_at is not None:
        queries = nt_dot(w_t[:C, :], normed).astype(BF16)
        q_ref[:, pl.ds(q_at, count)] = queries
        wide = queries.astype(F32)
        sums = nn_dot(head_pick(HEADS, C, 1), (wide * wide).astype(BF16))
        tall = jnp.max(sums, axis=0, keepdims=True)
        peak_ref[1:2, :] = jnp.maximum(peak_ref[1:2, :], jnp.maximum(tall[:, :CELL], tall[:, count - CELL :]))


def turn(qkv_ref, w_ref):
    for at, source in ((0, 0), (C, 2 * C)):
        w_ref[at : at + C, :] = qkv_ref[:, source : source + C].astype(F32).T.astype(BF16)


def attend(windows, pads, k_ref, v_ref, q_ref, m_ref, exact, unroll):
    def one_head(head):
        row = pl.multiple_of(head * HD, HD)
        half = pl.ds(pl.multiple_of((head // 8) * CELL, CELL), CELL)
        for q_lo, q_n, k_lo, k_n in windows:
            lane_head = lax.broadcasted_iota(I32, (CELL, q_n), 0) // HD
            queries = q_ref[half, q_lo : q_lo + q_n]
            queries = jnp.where(lane_head == head % 8, queries, jnp.zeros_like(queries))
            scores = nn_dot(k_ref[k_lo : k_lo + k_n, half], queries)
            if exact:
                scores = scores - jnp.max(scores, axis=0, keepdims=True)
            weights = jnp.exp2(scores * SCORE_SCALE)
            total = jnp.sum(jnp.sum(weights.reshape(k_n // 8, 8, q_n), axis=0), axis=0, keepdims=True)
            for cell in range(k_n // CELL):
                total = total - pads[k_lo // CELL + cell] * weights[cell * CELL : cell * CELL + 1, :]
            mixed = nn_dot(v_ref[pl.ds(row, HD), k_lo : k_lo + k_n], weights.astype(BF16))
            m_ref[pl.ds(row, HD), q_lo : q_lo + q_n] = (mixed / total).astype(BF16)

    def step(i, carry):
        for u in range(unroll):
            one_head(i * unroll + u)
        return carry

    lax.fori_loop(0, HEADS // unroll, step, 0)


def attend_any(windows, pads, peak_ref, k_ref, v_ref, q_ref, m_ref):
    bound = peak_ref[0:1, :] * peak_ref[1:2, :] * SCORE_SCALE**2
    off = (bound >= SAFE_EXPONENT * SAFE_EXPONENT) | (peak_ref[2:3, :] >= SAFE_VALUE)
    safe = jnp.max(jnp.where(off, 1.0, 0.0)) < 0.5

    @pl.when(safe)
    def _():
        attend(windows, pads, k_ref, v_ref, q_ref, m_ref, False, 4)

    @pl.when(jnp.logical_not(safe))
    def _():
        attend(windows, pads, k_ref, v_ref, q_ref, m_ref, True, 1)


def gelu(values):
    return 0.5 * values * (1.0 + lax.erf(values * (2.0**-0.5)))


def finish(rows, mixture_t, gain, offset, out_w, up_w, down_w):
    residual = rows.astype(F32) + nn_dot(mixture_t.astype(F32).T.astype(BF16), out_w)
    residual = residual.astype(BF16).astype(F32)
    normed = norm_rows_of(residual, gain, offset).astype(BF16)
    hidden = gelu(nn_dot(normed, up_w)).astype(BF16)
    return (residual + nn_dot(hidden, down_w)).astype(BF16)


def widest(peak_ref):
    peak_ref[...] = jnp.broadcast_to(jnp.max(peak_ref[...], axis=1, keepdims=True), peak_ref.shape)


def started(*pairs):
    copies = [pltpu.make_async_copy(*pair) for pair in pairs]
    for copy in copies:
        copy.start()
    return copies


def finished(copies):
    for copy in copies:
        copy.wait()


def gather_kernel(
    pos_hbm, count_hbm, x_hbm, norm_hbm, qkv_hbm,
    cells_ref, k_ref, v_ref, q_ref, meta_ref, peak_ref,
    pos_ref, count_ref, x_buf, norm_ref, out_buf, note_out, note_in, qkv_ref, w_ref,
    load_sem, x_sem, send, recv, note_send, note_recv,
):
    me, seq = lax.axis_index("grp"), lax.axis_index("seq")
    x_loads = started(*((x_hbm.at[j], x_buf.at[j], x_sem.at[j]) for j in range(CELLS)))
    loads = started(
        (pos_hbm, pos_ref, load_sem.at[0]), (count_hbm, count_ref, load_sem.at[1]),
        (norm_hbm, norm_ref, load_sem.at[2]), (qkv_hbm.at[0], qkv_ref, load_sem.at[3]),
    )

    def partner(i, sign):
        hop = i // 2
        hop = jnp.where(hop == 2, 3, jnp.where(hop == 3, 2, hop))
        chip = lax.rem(me // 2 + sign * hop + CELLS // 2, CELLS // 2)
        return chip * 2 + lax.rem(me + i, 2)

    barrier = pltpu.get_barrier_semaphore()
    for i in range(1, CELLS):
        pl.semaphore_signal(barrier, inc=1, device_id=(partner(i, 1), seq), device_id_type=MESH)
    finished(loads[:2])
    finished(x_loads)
    row = lax.broadcasted_iota(I32, (CELLS, CELL), 0)
    for owner in range(CELLS):
        index, place, count = jnp.int32(0), jnp.int32(0), jnp.int32(0)
        for j in range(CELLS):
            position = pos_ref[j]
            mine = position // CELLS == owner
            index = jnp.where(mine, j, index)
            place = jnp.where(mine, position % CELLS, place)
            count = jnp.where(mine, count_ref[j], count)
        out_buf[owner] = x_buf[index]
        note_out[owner] = jnp.where(row == 0, place, count)
    pl.semaphore_wait(barrier, CELLS - 1)

    def sent(i):
        owner = partner(i, 1)
        return (
            pltpu.make_async_remote_copy(
                out_buf.at[owner], cells_ref.at[me], send.at[i], recv.at[i],
                device_id=(owner, seq), device_id_type=MESH),
            pltpu.make_async_remote_copy(
                note_out.at[owner], note_in.at[me], note_send.at[i], note_recv.at[i],
                device_id=(owner, seq), device_id_type=MESH),
        )

    copies = [sent(i) for i in range(CELLS - 1, 0, -1)]
    for pair in copies:
        for copy in pair:
            copy.start()
    finished(loads[2:])
    turn(qkv_ref, w_ref)
    gain, offset = norm_ref[0, 0:1, :], norm_ref[0, 1:2, :]
    peak_ref[...] = jnp.zeros_like(peak_ref)

    def take(j):
        at = pl.multiple_of(j * CELL, CELL)
        count = note_in[j, 1:2, :]
        rows = first_valid(cells_ref[j].astype(F32), count[:, 0:1])
        project(
            rows, lane_valid(count), gain, offset, w_ref[...], qkv_ref[:, C : 2 * C],
            k_ref, v_ref, q_ref, peak_ref, at, at,
        )

    cells_ref[me] = out_buf[me]
    note_in[me] = note_out[me]
    take(me)

    def arrive(i, carry):
        for copy in sent(i):
            copy.wait_recv()
        take(partner(i, -1))
        return carry

    lax.fori_loop(1, CELLS, arrive, 0)
    lane = lax.broadcasted_iota(I32, (CELLS, CELL), 1)
    meta = jnp.zeros((CELLS, CELL), I32)
    for j in range(CELLS):
        meta = jnp.where(lane == j, note_in[j], meta)
    meta_ref[...] = meta
    widest(peak_ref)
    for pair in copies:
        for copy in pair:
            copy.wait_send()


def vmem():
    return pl.BlockSpec(memory_space=pltpu.VMEM)


def hbm():
    return pl.BlockSpec(memory_space=pltpu.HBM)


def shape(dims, dtype=BF16):
    return jax.ShapeDtypeStruct(dims, dtype)


def dma(*dims):
    return pltpu.SemaphoreType.DMA(dims)


def gather_cells(pos, counts, cells, norms, qkv):
    return pl.pallas_call(
        gather_kernel,
        out_shape=(
            shape((CELLS, CELL, C)), shape((ROWS, C)), shape((C, ROWS)), shape((C, ROWS)),
            shape((CELLS, CELL), I32), shape((CELLS, CELL), F32),
        ),
        in_specs=[hbm()] * 5,
        out_specs=(vmem(),) * 6,
        scratch_shapes=[
            pltpu.SMEM((CELLS,), I32),
            pltpu.SMEM((CELLS,), I32),
            pltpu.VMEM((CELLS, CELL, C), BF16),
            pltpu.VMEM((2, 4, C), F32),
            pltpu.VMEM((CELLS, CELL, C), BF16),
            pltpu.VMEM((CELLS, CELLS, CELL), I32),
            pltpu.VMEM((CELLS, CELLS, CELL), I32),
            pltpu.VMEM((C, 3 * C), BF16),
            pltpu.VMEM((2 * C, C), BF16),
            dma(4), dma(CELLS), dma(CELLS), dma(CELLS), dma(CELLS), dma(CELLS),
        ],
        compiler_params=pltpu.CompilerParams(
            collective_id=0, has_side_effects=True, vmem_limit_bytes=24 * 2**20),
        name="gather_cells",
    )(pos, counts, cells, norms, qkv)


def aligned_kernel(
    meta_ref, peak_ref, k_ref, v_ref, q_ref, cells_ref, m_ref, placed_ref, count_ref,
    place_ref, mix_ref, sem,
):
    loads = started((meta_ref, place_ref, sem.at[0]))
    pads = [(CELL - meta_ref[1:2, j : j + 1]).astype(F32) for j in range(CELLS)]
    attend_any(((0, HALF, 0, ROWS), (HALF, HALF, 0, ROWS)), pads, peak_ref, k_ref, v_ref, q_ref, mix_ref)
    finished(loads)
    for j in range(CELLS):
        to = place_ref[0, j]
        m_ref[:, pl.ds(pl.multiple_of(to * CELL, CELL), CELL)] = mix_ref[:, j * CELL : (j + 1) * CELL]
        placed_ref[to] = cells_ref[j]
        count_ref[pl.ds(to, 1), :] = jnp.full((1, CELL), place_ref[1, j], I32)


def aligned_attention(meta, peak, keys, values, queries, cells):
    return pl.pallas_call(
        aligned_kernel,
        out_shape=(shape((C, ROWS)), shape((CELLS, CELL, C)), shape((CELLS, CELL), I32)),
        in_specs=[vmem()] * 6,
        out_specs=(vmem(),) * 3,
        scratch_shapes=[
            pltpu.SMEM((CELLS, CELL), I32),
            pltpu.VMEM((C, ROWS), BF16),
            dma(1),
        ],
        compiler_params=pltpu.CompilerParams(vmem_limit_bytes=40 * 2**20),
        name="aligned_attention",
    )(meta, peak, keys, values, queries, cells)


def along(step):
    n_grp, n_seq = lax.axis_size("grp"), lax.axis_size("seq")
    flat = lax.axis_index("grp") * n_seq + lax.axis_index("seq")
    other = lax.rem(flat + step + n_grp * n_seq, n_grp * n_seq)
    return (other // n_seq, lax.rem(other, n_seq))


def middle_kernel(
    note_ref, x_ref, m_ref, norm_ref, qkv_ref, out_ref, up_ref, down_ref,
    y_ref, k_ref, v_ref, q_ref, all_count_ref, peak_ref,
    before_ref, after_ref, note_before, note_after, w_ref,
    send_before, send_after, recv_before, recv_after, note_send, note_recv,
):
    after, before = along(1), along(-1)
    barrier = pltpu.get_barrier_semaphore()
    for device in (after, before):
        pl.semaphore_signal(barrier, inc=1, device_id=device, device_id_type=MESH)
    turn(qkv_ref.at[1], w_ref)
    gain, offset = norm_ref[1, 0:1, :], norm_ref[1, 1:2, :]
    peak_ref[...] = jnp.zeros_like(peak_ref)
    notes = [
        pltpu.make_async_remote_copy(
            note_ref, target, note_send.at[i], note_recv.at[i], device_id=device, device_id_type=MESH)
        for i, (target, device) in enumerate(((note_after, before), (note_before, after)))
    ]

    def to_before(i):
        return pltpu.make_async_remote_copy(
            y_ref.at[pl.ds(i * STEP, STEP)], after_ref.at[pl.ds(i * STEP, STEP)],
            send_before.at[i], recv_after.at[i], device_id=before, device_id_type=MESH)

    def to_after(i):
        return pltpu.make_async_remote_copy(
            y_ref.at[pl.ds(HALF + i * STEP, STEP)], before_ref.at[pl.ds(i * STEP, STEP)],
            send_after.at[i], recv_before.at[i], device_id=after, device_id_type=MESH)

    def place(rows, pair, k_at, q_at):
        wide = rows.astype(F32)
        wide = jnp.concatenate(
            [first_valid(wide[u * CELL : (u + 1) * CELL], pair[u]) for u in range(2)], axis=0)
        valid = jnp.concatenate([lane_valid(pair[u]) for u in range(2)], axis=1)
        project(
            wide, valid, gain, offset, w_ref[...], qkv_ref[1, :, C : 2 * C],
            k_ref, v_ref, q_ref, peak_ref, k_at, q_at,
        )

    for i in range(2):
        for chunk, copy in ((i, to_before(i)), (2 + i, to_after(i))):
            at = chunk * STEP
            cells = (2 * chunk, 2 * chunk + 1)
            done = finish(
                jnp.concatenate([x_ref[p] for p in cells], axis=0), m_ref[:, at : at + STEP],
                norm_ref[0, 2:3, :], norm_ref[0, 3:4, :], out_ref[0], up_ref[0], down_ref[0],
            )
            y_ref[at : at + STEP, :] = done
            place(done, [note_ref[p : p + 1, 0:1] for p in cells], HALF + at, at)
            if i == 0 and chunk == 0:
                pl.semaphore_wait(barrier, 2)
                for note in notes:
                    note.start()
            copy.start()
    for copy in notes:
        copy.wait()
    for i in range(2):
        for incoming, source, note, first, k_first in (
            (to_before(i), after_ref, note_after, 2 * i, HALF + ROWS),
            (to_after(i), before_ref, note_before, CELLS // 2 + 2 * i, 0),
        ):
            incoming.wait_recv()
            pair = [note[first + u : first + u + 1, 0:1] for u in range(2)]
            place(source[i * STEP : (i + 1) * STEP, :], pair, k_first + i * STEP, None)
    all_count_ref[0:4, :] = note_before[4:8, :]
    all_count_ref[4:12, :] = note_ref[...]
    all_count_ref[12:16, :] = note_after[0:4, :]
    widest(peak_ref)
    for i in range(2):
        to_before(i).wait_send()
        to_after(i).wait_send()


def middle(notes, cells, mixture, norms, qkv, out_w, up_w, down_w):
    return pl.pallas_call(
        middle_kernel,
        out_shape=(
            shape((ROWS, C)), shape((2 * ROWS, C)), shape((C, 2 * ROWS)), shape((C, ROWS)),
            shape((2 * CELLS, CELL), I32), shape((CELLS, CELL), F32),
        ),
        in_specs=[vmem()] * 8,
        out_specs=(vmem(),) * 6,
        scratch_shapes=[
            pltpu.VMEM((HALF, C), BF16),
            pltpu.VMEM((HALF, C), BF16),
            pltpu.VMEM((CELLS, CELL), I32),
            pltpu.VMEM((CELLS, CELL), I32),
            pltpu.VMEM((2 * C, C), BF16),
            dma(2), dma(2), dma(2), dma(2), dma(2), dma(2),
        ],
        compiler_params=pltpu.CompilerParams(
            collective_id=1, has_side_effects=True, vmem_limit_bytes=32 * 2**20),
        name="middle",
    )(notes, cells, mixture, norms, qkv, out_w, up_w, down_w)


def shifted_kernel(
    count_ref, peak_ref, k_ref, v_ref, q_ref, x_ref, norm_ref, out_ref, up_ref, down_ref,
    y_hbm, m_ref, y_ref, store_sem,
):
    pads = [(CELL - count_ref[j : j + 1, 0:1]).astype(F32) for j in range(2 * CELLS)]
    attend_any(((0, HALF, 0, ROWS), (HALF, HALF, ROWS, ROWS)), pads, peak_ref, k_ref, v_ref, q_ref, m_ref)
    stores = []
    for i in range(ROWS // STEP):
        at = i * STEP
        done = finish(
            x_ref[at : at + STEP, :], m_ref[:, at : at + STEP], norm_ref[1, 2:3, :], norm_ref[1, 3:4, :],
            out_ref[1], up_ref[1], down_ref[1],
        )
        for u in range(2):
            cell = CELLS // 2 + 2 * i + u
            keep = lax.broadcasted_iota(I32, (CELL, 1), 0) < count_ref[cell : cell + 1, 0:1]
            part = done[u * CELL : (u + 1) * CELL, :]
            y_ref[at + u * CELL : at + (u + 1) * CELL, :] = jnp.where(keep, part, jnp.zeros_like(part))
        rows = pl.ds(at, STEP)
        stores += started((y_ref.at[rows], y_hbm.at[rows], store_sem.at[i]))
    finished(stores)


def shifted_block(counts, peak, keys, values, queries, rows, norms, out_w, up_w, down_w):
    return pl.pallas_call(
        shifted_kernel,
        out_shape=shape((ROWS, C)),
        in_specs=[vmem()] * 10,
        out_specs=hbm(),
        scratch_shapes=[
            pltpu.VMEM((C, ROWS), BF16),
            pltpu.VMEM((ROWS, C), BF16),
            dma(4),
        ],
        compiler_params=pltpu.CompilerParams(vmem_limit_bytes=40 * 2**20),
        name="shifted_block",
    )(counts, peak, keys, values, queries, rows, norms, out_w, up_w, down_w)


def body(points, hilbert_pos, valid_counts, norms, qkv, out_w, up_w, down_w):
    cells, keys, values, queries, meta, peak = gather_cells(*(
        pltpu.with_memory_space_constraint(array, pltpu.HBM)
        for array in (hilbert_pos, valid_counts, points.reshape(CELLS, CELL, C), norms, qkv)))
    mixture, placed, notes = aligned_attention(meta, peak, keys, values, queries, cells)
    rows, keys, values, queries, counts, peak = middle(notes, placed, mixture, norms, qkv, out_w, up_w, down_w)
    return shifted_block(counts, peak, keys, values, queries, rows, norms, out_w, up_w, down_w)


def solution(mesh):
    return jax.shard_map(
        body,
        mesh=mesh,
        in_specs=(
            P(("grp", "seq"), None), P(("grp", "seq")), P(("grp", "seq")), P(), P(), P(), P(), P(),
        ),
        out_specs=P(("grp", "seq"), None),
        check_vma=False,
    )
```

time: 99.6 us -> 95 us (0.954)
  local copies, waits for them, and re-layouts: 3.57 us -> 0.03 us
  Pallas kernels: 95.6 us -> 94.6 us
    unnamed x20 -> x10, local copies, waits for them, and re-layouts: 3.57 us -> 0.03 us
    pallas_call x1, Pallas kernels: 28.1 us -> 26.7 us  [aligned_attention(): pl.pallas_call(aligned_kernel, out_shape=(shape((C, ROWS)), shape((CELLS,...]
    pallas_call x1, Pallas kernels: 30.6 us -> 32 us  [shifted_block(): pl.pallas_call(shifted_kernel, out_shape=shape((ROWS, C)), in_specs=[vmem...]
where the time goes in v1:
time: 95 us; the launch traced here: 94.9 us
  Pallas kernels  94.6 us (100%)
    pallas_call x1, Pallas kernels, shifted_block(): pl.pallas_call(shifted_kernel, out_shape=shape((ROWS, C)), in_specs=[vmem...  32 us
    pallas_call x1, Pallas kernels, aligned_attention(): pl.pallas_call(aligned_kernel, out_shape=(shape((C, ROWS)), shape((CELLS,...  26.7 us
    pallas_call x1, Pallas kernels, middle(): pl.pallas_call(middle_kernel, out_shape=(shape((ROWS, C)), shape((2 * ROW...  18.5 us
    pallas_call x1, Pallas kernels, gather_cells(): pl.pallas_call(gather_kernel, out_shape=(shape((CELLS, CELL, C)), shape((...  17.4 us

profile of v1, /device:TPU:1, one launch (start us, length us, event | category | flops | bytes accessed | tf_op | source)
XLA Modules:
  0.0 94.9 jit_solution(3276053945275843912)
XLA Ops:
  0.0 0.0 copy-start.2
  0.0 0.0 copy-start.3
  0.0 17.4 %gather_cells.1 = (bf16[8,128,256]{2,1,0:T(8,128)(2,1)S(1)}, bf16[1024,256]{1,0:T(8,128)(2,1)S(1)}, bf16[256,1024]{1,0:T(8,128)(2,1)S(1)}, bf16[256,1024]{1,0:T(...) custom-call(s32[8]{0:T(128)} %pos_hbm.1, s32[8]{0:T(128)} %count_hbm.1, bf16[8,128,256]{2,1,0:T(8,128)(2,1)} %bitcast.1, ...), custom_call_target="tpu_custom_call" | custom-call | tf_op jit(solution)/shard_map/gather_cells/pallas_call | solution.py:257
  17.5 0.0 copy-start
  17.5 0.0 copy-start.1
  17.5 0.0 copy-start.4
  17.5 26.7 %aligned_attention.1 = (bf16[256,1024]{1,0:T(8,128)(2,1)S(1)}, bf16[8,128,256]{2,1,0:T(8,128)(2,1)S(1)}, s32[8,128]{1,0:T(8,128)S(1)}) custom-call(s32[8,128]{1,0:T(8,128)S(1)} %get-tuple-element.20.meta_ref, f32[8,128]{1,0:T(8,128)S(1)} %get-tuple-element.21.peak_ref, bf16[1024,256]{1,0:T(8,128)(2,1)S(1)} %get-tuple-element.22.k_ref, ...), custom_call_target="tpu_custom_call" | custom-call | tf_op jit(solution)/shard_map/aligned_attention/pallas_call | solution.py:299
  44.2 0.0 copy-done.2
  44.2 0.0 copy-done.3
  44.2 0.0 copy-done
  44.2 0.0 copy-done.1
  44.2 0.0 copy-done.4
  44.3 18.5 %middle.1 = (bf16[1024,256]{1,0:T(8,128)(2,1)S(1)}, bf16[2048,256]{1,0:T(8,128)(2,1)S(1)}, bf16[256,2048]{1,0:T(8,128)(2,1)S(1)}, bf16[256,1024]{1,0:T(8,128)(2,...) custom-call(s32[8,128]{1,0:T(8,128)S(1)} %get-tuple-element.26.note_ref, ...), custom_call_target="tpu_custom_call" | custom-call | tf_op jit(solution)/shard_map/middle/pallas_call | solution.py:395
  62.8 32.0 %shifted_block.1 = bf16[1024,256]{1,0:T(8,128)(2,1)} custom-call(s32[16,128]{1,0:T(8,128)S(1)} %get-tuple-element.29.count_ref, f32[8,128]{1,0:T(8,128)S(1)} %get-tuple-element.30.peak_ref, bf16[2048,256]{1,0:T(8,128)(2,1)S(1)} %get-tuple-element.31.k_ref, bf16[256,2048]{1,0:T(8,128)(2,1)S(1)} %get-tuple-element.32.v_ref, ...), custom_call_target="tpu_custom_call" | custom-call | tf_op jit(solution)/shard_map/shifted_block/pallas_call | solution.py:441
Async XLA Ops:
  0.0 44.2 %copy-start.2 = (bf16[2,256,768]{2,1,0:T(8,128)(2,1)S(1)}, bf16[2,256,768]{2,1,0:T(8,128)(2,1)}, u32[]{:S(2)}) copy-start(bf16[2,256,768]{2,1,0:T(8,128)(2,1)} %qkv_ref.1) | copy-start | bytes 2359300
  0.0 44.2 %copy-start.3 = (bf16[2,256,256]{2,1,0:T(8,128)(2,1)S(1)}, bf16[2,256,256]{2,1,0:T(8,128)(2,1)}, u32[]{:S(2)}) copy-start(bf16[2,256,256]{2,1,0:T(8,128)(2,1)} %out_ref.3) | copy-start | bytes 786436
  17.5 26.8 %copy-start = (bf16[2,256,1024]{2,1,0:T(8,128)(2,1)S(1)}, bf16[2,256,1024]{2,1,0:T(8,128)(2,1)}, u32[]{:S(2)}) copy-start(bf16[2,256,1024]{2,1,0:T(8,128)(2,1)} %up_ref.3) | copy-start | bytes 3145732
  17.5 26.8 %copy-start.1 = (bf16[2,1024,256]{2,1,0:T(8,128)(2,1)S(1)}, bf16[2,1024,256]{2,1,0:T(8,128)(2,1)}, u32[]{:S(2)}) copy-start(bf16[2,1024,256]{2,1,0:T(8,128)(2,1)} %down_ref.3) | copy-start | bytes 3145732
  17.5 26.8 %copy-start.4 = (f32[2,4,256]{2,1,0:T(4,128)S(1)}, f32[2,4,256]{2,1,0:T(4,128)}, u32[]{:S(2)}) copy-start(f32[2,4,256]{2,1,0:T(4,128)} %norm_ref.3) | copy-start | bytes 24580

commit v2 on v1

--- a/solution.py
+++ b/solution.py
@@ -23,6 +23,13 @@
 SCORE_SCALE = HD**-0.5 * math.log2(math.e)
 SAFE_EXPONENT = 60.0
 SAFE_VALUE = 2.0**40
+UNROLL = 4
+EARLY = ((0, HALF, 0, HALF, False, False),)
+LATE = ((0, HALF, HALF, HALF, True, True), (HALF, HALF, 0, ROWS, False, True))
+ALIGNED = ((0, HALF, 0, ROWS, False, True), (HALF, HALF, 0, ROWS, False, True))
+OWN = ((0, HALF, HALF, HALF, False, False), (HALF, HALF, ROWS, HALF, False, False))
+BORROWED = ((0, HALF, 0, HALF, True, True), (HALF, HALF, ROWS + HALF, HALF, True, True))
+SHIFTED = ((0, HALF, 0, ROWS, False, True), (HALF, HALF, ROWS, ROWS, False, True))
 
 
 def nt_dot(a, b):
@@ -81,13 +88,14 @@
         w_ref[at : at + C, :] = qkv_ref[:, source : source + C].astype(F32).T.astype(BF16)
 
 
-def attend(windows, pads, k_ref, v_ref, q_ref, m_ref, exact, unroll):
+def attend(windows, pads, k_ref, v_ref, q_ref, m_ref, part, exact, unroll):
     def one_head(head):
-        row = pl.multiple_of(head * HD, HD)
+        row = pl.ds(pl.multiple_of(head * HD, HD), HD)
         half = pl.ds(pl.multiple_of((head // 8) * CELL, CELL), CELL)
-        for q_lo, q_n, k_lo, k_n in windows:
+        for q_lo, q_n, k_lo, k_n, goes_on, ends in windows:
+            q_at = pl.ds(q_lo, q_n)
             lane_head = lax.broadcasted_iota(I32, (CELL, q_n), 0) // HD
-            queries = q_ref[half, q_lo : q_lo + q_n]
+            queries = q_ref[half, q_at]
             queries = jnp.where(lane_head == head % 8, queries, jnp.zeros_like(queries))
             scores = nn_dot(k_ref[k_lo : k_lo + k_n, half], queries)
             if exact:
@@ -96,8 +104,15 @@
             total = jnp.sum(jnp.sum(weights.reshape(k_n // 8, 8, q_n), axis=0), axis=0, keepdims=True)
             for cell in range(k_n // CELL):
                 total = total - pads[k_lo // CELL + cell] * weights[cell * CELL : cell * CELL + 1, :]
-            mixed = nn_dot(v_ref[pl.ds(row, HD), k_lo : k_lo + k_n], weights.astype(BF16))
-            m_ref[pl.ds(row, HD), q_lo : q_lo + q_n] = (mixed / total).astype(BF16)
+            mixed = nn_dot(v_ref[row, k_lo : k_lo + k_n], weights.astype(BF16))
+            if goes_on:
+                mixed = mixed + part[0][row, q_at]
+                total = total + part[1][pl.ds(head, 1), q_at]
+            if ends:
+                m_ref[row, q_at] = (mixed / total).astype(BF16)
+            else:
+                part[0][row, q_at] = mixed
+                part[1][pl.ds(head, 1), q_at] = total
 
     def step(i, carry):
         for u in range(unroll):
@@ -107,18 +122,18 @@
     lax.fori_loop(0, HEADS // unroll, step, 0)
 
 
-def attend_any(windows, pads, peak_ref, k_ref, v_ref, q_ref, m_ref):
+def attend_any(windows, whole_windows, pads, peak_ref, k_ref, v_ref, q_ref, m_ref, part):
     bound = peak_ref[0:1, :] * peak_ref[1:2, :] * SCORE_SCALE**2
     off = (bound >= SAFE_EXPONENT * SAFE_EXPONENT) | (peak_ref[2:3, :] >= SAFE_VALUE)
     safe = jnp.max(jnp.where(off, 1.0, 0.0)) < 0.5
 
     @pl.when(safe)
     def _():
-        attend(windows, pads, k_ref, v_ref, q_ref, m_ref, False, 4)
+        attend(windows, pads, k_ref, v_ref, q_ref, m_ref, part, False, UNROLL)
 
     @pl.when(jnp.logical_not(safe))
     def _():
-        attend(windows, pads, k_ref, v_ref, q_ref, m_ref, True, 1)
+        attend(whole_windows, pads, k_ref, v_ref, q_ref, m_ref, part, True, 1)
 
 
 def gelu(values):
@@ -151,7 +166,7 @@
 
 def gather_kernel(
     pos_hbm, count_hbm, x_hbm, norm_hbm, qkv_hbm,
-    cells_ref, k_ref, v_ref, q_ref, meta_ref, peak_ref,
+    cells_ref, k_ref, v_ref, q_ref, meta_ref, peak_ref, mixed_ref, total_ref,
     pos_ref, count_ref, x_buf, norm_ref, out_buf, note_out, note_in, qkv_ref, w_ref,
     load_sem, x_sem, send, recv, note_send, note_recv,
 ):
@@ -162,15 +177,14 @@
         (norm_hbm, norm_ref, load_sem.at[2]), (qkv_hbm.at[0], qkv_ref, load_sem.at[3]),
     )
 
-    def partner(i, sign):
+    def partner(i):
         hop = i // 2
-        hop = jnp.where(hop == 2, 3, jnp.where(hop == 3, 2, hop))
-        chip = lax.rem(me // 2 + sign * hop + CELLS // 2, CELLS // 2)
-        return chip * 2 + lax.rem(me + i, 2)
+        hop = 3 if hop == 2 else 2 if hop == 3 else hop
+        return lax.rem(me // 2 + hop, CELLS // 2) * 2 + lax.rem(me + i, 2)
 
     barrier = pltpu.get_barrier_semaphore()
     for i in range(1, CELLS):
-        pl.semaphore_signal(barrier, inc=1, device_id=(partner(i, 1), seq), device_id_type=MESH)
+        pl.semaphore_signal(barrier, inc=1, device_id=(partner(i), seq), device_id_type=MESH)
     finished(loads[:2])
     finished(x_loads)
     row = lax.broadcasted_iota(I32, (CELLS, CELL), 0)
@@ -187,18 +201,18 @@
     pl.semaphore_wait(barrier, CELLS - 1)
 
     def sent(i):
-        owner = partner(i, 1)
+        owner = partner(i)
         return (
             pltpu.make_async_remote_copy(
-                out_buf.at[owner], cells_ref.at[me], send.at[i], recv.at[i],
+                out_buf.at[owner], cells_ref.at[i], send.at[i], recv.at[i],
                 device_id=(owner, seq), device_id_type=MESH),
             pltpu.make_async_remote_copy(
-                note_out.at[owner], note_in.at[me], note_send.at[i], note_recv.at[i],
+                note_out.at[owner], note_in.at[i], note_send.at[i], note_recv.at[i],
                 device_id=(owner, seq), device_id_type=MESH),
         )
 
-    copies = [sent(i) for i in range(CELLS - 1, 0, -1)]
-    for pair in copies:
+    copies = [sent(i) for i in range(1, CELLS)]
+    for pair in copies[:5]:
         for copy in pair:
             copy.start()
     finished(loads[2:])
@@ -215,24 +229,35 @@
             k_ref, v_ref, q_ref, peak_ref, at, at,
         )
 
-    cells_ref[me] = out_buf[me]
-    note_in[me] = note_out[me]
-    take(me)
-
-    def arrive(i, carry):
-        for copy in sent(i):
+    cells_ref[0] = out_buf[me]
+    note_in[0] = note_out[me]
+    take(0)
+
+    def arrive(i):
+        for copy in copies[i - 1]:
             copy.wait_recv()
-        take(partner(i, -1))
-        return carry
-
-    lax.fori_loop(1, CELLS, arrive, 0)
+        take(i)
+
+    arrive(1)
+    for pair in copies[:5]:
+        for copy in pair:
+            copy.wait_send()
+    for pair in copies[5:]:
+        for copy in pair:
+            copy.start()
+    arrive(2)
+    arrive(3)
+    pads = [(CELL - note_in[j, 1:2, 0:1]).astype(F32) for j in range(CELLS // 2)]
+    attend(EARLY, pads, k_ref, v_ref, q_ref, None, (mixed_ref, total_ref), False, UNROLL)
+    for i in range(4, CELLS):
+        arrive(i)
     lane = lax.broadcasted_iota(I32, (CELLS, CELL), 1)
     meta = jnp.zeros((CELLS, CELL), I32)
     for j in range(CELLS):
         meta = jnp.where(lane == j, note_in[j], meta)
     meta_ref[...] = meta
     widest(peak_ref)
-    for pair in copies:
+    for pair in copies[5:]:
         for copy in pair:
             copy.wait_send()
 
@@ -258,10 +283,10 @@
         gather_kernel,
         out_shape=(
             shape((CELLS, CELL, C)), shape((ROWS, C)), shape((C, ROWS)), shape((C, ROWS)),
-            shape((CELLS, CELL), I32), shape((CELLS, CELL), F32),
+            shape((CELLS, CELL), I32), shape((CELLS, CELL), F32), shape((C, HALF), F32), shape((HEADS, HALF), F32),
         ),
         in_specs=[hbm()] * 5,
-        out_specs=(vmem(),) * 6,
+        out_specs=(vmem(),) * 8,
         scratch_shapes=[
             pltpu.SMEM((CELLS,), I32),
             pltpu.SMEM((CELLS,), I32),
@@ -275,18 +300,18 @@
             dma(4), dma(CELLS), dma(CELLS), dma(CELLS), dma(CELLS), dma(CELLS),
         ],
         compiler_params=pltpu.CompilerParams(
-            collective_id=0, has_side_effects=True, vmem_limit_bytes=24 * 2**20),
+            collective_id=0, has_side_effects=True, vmem_limit_bytes=32 * 2**20),
         name="gather_cells",
     )(pos, counts, cells, norms, qkv)
 
 
 def aligned_kernel(
-    meta_ref, peak_ref, k_ref, v_ref, q_ref, cells_ref, m_ref, placed_ref, count_ref,
+    meta_ref, peak_ref, k_ref, v_ref, q_ref, cells_ref, mixed_ref, total_ref, m_ref, placed_ref, count_ref,
     place_ref, mix_ref, sem,
 ):
     loads = started((meta_ref, place_ref, sem.at[0]))
     pads = [(CELL - meta_ref[1:2, j : j + 1]).astype(F32) for j in range(CELLS)]
-    attend_any(((0, HALF, 0, ROWS), (HALF, HALF, 0, ROWS)), pads, peak_ref, k_ref, v_ref, q_ref, mix_ref)
+    attend_any(LATE, ALIGNED, pads, peak_ref, k_ref, v_ref, q_ref, mix_ref, (mixed_ref, total_ref))
     finished(loads)
     for j in range(CELLS):
         to = place_ref[0, j]
@@ -295,20 +320,20 @@
         count_ref[pl.ds(to, 1), :] = jnp.full((1, CELL), place_ref[1, j], I32)
 
 
-def aligned_attention(meta, peak, keys, values, queries, cells):
+def aligned_attention(meta, peak, keys, values, queries, cells, mixed, total):
     return pl.pallas_call(
         aligned_kernel,
         out_shape=(shape((C, ROWS)), shape((CELLS, CELL, C)), shape((CELLS, CELL), I32)),
-        in_specs=[vmem()] * 6,
+        in_specs=[vmem()] * 8,
         out_specs=(vmem(),) * 3,
         scratch_shapes=[
             pltpu.SMEM((CELLS, CELL), I32),
             pltpu.VMEM((C, ROWS), BF16),
             dma(1),
         ],
-        compiler_params=pltpu.CompilerParams(vmem_limit_bytes=40 * 2**20),
+        compiler_params=pltpu.CompilerParams(vmem_limit_bytes=36 * 2**20),
         name="aligned_attention",
-    )(meta, peak, keys, values, queries, cells)
+    )(meta, peak, keys, values, queries, cells, mixed, total)
 
 
 def along(step):
@@ -320,7 +345,7 @@
 
 def middle_kernel(
     note_ref, x_ref, m_ref, norm_ref, qkv_ref, out_ref, up_ref, down_ref,
-    y_ref, k_ref, v_ref, q_ref, all_count_ref, peak_ref,
+    y_ref, k_ref, v_ref, q_ref, all_count_ref, peak_ref, mixed_ref, total_ref,
     before_ref, after_ref, note_before, note_after, w_ref,
     send_before, send_after, recv_before, recv_after, note_send, note_recv,
 ):
@@ -372,6 +397,8 @@
                 for note in notes:
                     note.start()
             copy.start()
+    pads = [None] * 4 + [(CELL - note_ref[p : p + 1, 0:1]).astype(F32) for p in range(CELLS)]
+    attend(OWN, pads, k_ref, v_ref, q_ref, None, (mixed_ref, total_ref), False, UNROLL)
     for copy in notes:
         copy.wait()
     for i in range(2):
@@ -396,10 +423,10 @@
         middle_kernel,
         out_shape=(
             shape((ROWS, C)), shape((2 * ROWS, C)), shape((C, 2 * ROWS)), shape((C, ROWS)),
-            shape((2 * CELLS, CELL), I32), shape((CELLS, CELL), F32),
+            shape((2 * CELLS, CELL), I32), shape((CELLS, CELL), F32), shape((C, ROWS), F32), shape((HEADS, ROWS), F32),
         ),
         in_specs=[vmem()] * 8,
-        out_specs=(vmem(),) * 6,
+        out_specs=(vmem(),) * 8,
         scratch_shapes=[
             pltpu.VMEM((HALF, C), BF16),
             pltpu.VMEM((HALF, C), BF16),
@@ -415,11 +442,11 @@
 
 
 def shifted_kernel(
-    count_ref, peak_ref, k_ref, v_ref, q_ref, x_ref, norm_ref, out_ref, up_ref, down_ref,
+    count_ref, peak_ref, k_ref, v_ref, q_ref, mixed_ref, total_ref, x_ref, norm_ref, out_ref, up_ref, down_ref,
     y_hbm, m_ref, y_ref, store_sem,
 ):
     pads = [(CELL - count_ref[j : j + 1, 0:1]).astype(F32) for j in range(2 * CELLS)]
-    attend_any(((0, HALF, 0, ROWS), (HALF, HALF, ROWS, ROWS)), pads, peak_ref, k_ref, v_ref, q_ref, m_ref)
+    attend_any(BORROWED, SHIFTED, pads, peak_ref, k_ref, v_ref, q_ref, m_ref, (mixed_ref, total_ref))
     stores = []
     for i in range(ROWS // STEP):
         at = i * STEP
@@ -437,29 +464,30 @@
     finished(stores)
 
 
-def shifted_block(counts, peak, keys, values, queries, rows, norms, out_w, up_w, down_w):
+def shifted_block(counts, peak, keys, values, queries, mixed, total, rows, norms, out_w, up_w, down_w):
     return pl.pallas_call(
         shifted_kernel,
         out_shape=shape((ROWS, C)),
-        in_specs=[vmem()] * 10,
+        in_specs=[vmem()] * 12,
         out_specs=hbm(),
         scratch_shapes=[
             pltpu.VMEM((C, ROWS), BF16),
             pltpu.VMEM((ROWS, C), BF16),
             dma(4),
         ],
-        compiler_params=pltpu.CompilerParams(vmem_limit_bytes=40 * 2**20),
+        compiler_params=pltpu.CompilerParams(vmem_limit_bytes=36 * 2**20),
         name="shifted_block",
-    )(counts, peak, keys, values, queries, rows, norms, out_w, up_w, down_w)
+    )(counts, peak, keys, values, queries, mixed, total, rows, norms, out_w, up_w, down_w)
 
 
 def body(points, hilbert_pos, valid_counts, norms, qkv, out_w, up_w, down_w):
-    cells, keys, values, queries, meta, peak = gather_cells(*(
+    cells, keys, values, queries, meta, peak, mixed, total = gather_cells(*(
         pltpu.with_memory_space_constraint(array, pltpu.HBM)
         for array in (hilbert_pos, valid_counts, points.reshape(CELLS, CELL, C), norms, qkv)))
-    mixture, placed, notes = aligned_attention(meta, peak, keys, values, queries, cells)
-    rows, keys, values, queries, counts, peak = middle(notes, placed, mixture, norms, qkv, out_w, up_w, down_w)
-    return shifted_block(counts, peak, keys, values, queries, rows, norms, out_w, up_w, down_w)
+    mixture, placed, notes = aligned_attention(meta, peak, keys, values, queries, cells, mixed, total)
+    rows, keys, values, queries, counts, peak, mixed, total = middle(notes, placed, mixture, norms, qkv, out_w, up_w, down_w)
+    return shifted_block(
+        counts, peak, keys, values, queries, mixed, total, rows, norms, out_w, up_w, down_w)
 
 
 def solution(mesh):

time: 95 us -> 103 us (1.084)
  Pallas kernels: 94.6 us -> 102 us
    pallas_call x1, Pallas kernels: 18.5 us -> 25 us  [middle(): pl.pallas_call(middle_kernel, out_shape=(shape((ROWS, C)), shape((2 * ROW...]
    pallas_call x1, Pallas kernels: 17.4 us -> 18.9 us  [gather_cells(): pl.pallas_call(gather_kernel, out_shape=(shape((CELLS, CELL, C)), shape((...]
where the time goes in v2:
time: 103 us
  Pallas kernels  102 us (99%)
    pallas_call x1, Pallas kernels, shifted_block(): pl.pallas_call(shifted_kernel, out_shape=shape((ROWS, C)), in_specs=[vmem...  32 us
    pallas_call x1, Pallas kernels, aligned_attention(): pl.pallas_call(aligned_kernel, out_shape=(shape((C, ROWS)), shape((CELLS,...  26.6 us
    pallas_call x1, Pallas kernels, middle(): pl.pallas_call(middle_kernel, out_shape=(shape((ROWS, C)), shape((2 * ROW...  25 us
    pallas_call x1, Pallas kernels, gather_cells(): pl.pallas_call(gather_kernel, out_shape=(shape((CELLS, CELL, C)), shape((...  18.9 us

profile of v2, /device:TPU:1, one launch (start us, length us, event | category | flops | bytes accessed | tf_op | source)
XLA Modules:
  0.0 102.8 jit_solution(2485937215814919428)
XLA Ops:
  0.0 0.0 copy-start.2
  0.0 18.9 %gather_cells.1 = (bf16[8,128,256]{2,1,0:T(8,128)(2,1)S(1)}, bf16[1024,256]{1,0:T(8,128)(2,1)S(1)}, bf16[256,1024]{1,0:T(8,128)(2,1)S(1)}, bf16[256,1024]{1,0:T(...) custom-call(s32[8]{0:T(128)} %pos_hbm.1, ...), custom_call_target="tpu_custom_call" | custom-call | tf_op jit(solution)/shard_map/gather_cells/pallas_call | solution.py:282
  18.9 0.0 copy-start
  18.9 0.0 copy-start.1
  18.9 0.0 copy-start.3
  18.9 0.0 copy-start.4
  19.0 26.6 %aligned_attention.1 = (bf16[256,1024]{1,0:T(8,128)(2,1)S(1)}, bf16[8,128,256]{2,1,0:T(8,128)(2,1)S(1)}, s32[8,128]{1,0:T(8,128)S(1)}) custom-call(s32[8,128]{1,0:T(8,128)S(1)} %get-tuple-element.24.meta_ref, f32[8,128]{1,0:T(8,128)S(1)} %get-tuple-element.25.peak_ref, bf16[1024,256]{1,0:T(8,128)(2,1)S(1)} %get-tuple-element.26.k_ref, ...), custom_call_target="tpu_custom_call" | custom-call | tf_op jit(solution)/shard_map/aligned_attention/pallas_call | solution.py:324
  45.6 0.0 copy-done.2
  45.6 0.0 copy-done
  45.6 0.0 copy-done.1
  45.6 0.0 copy-done.3
  45.6 0.0 copy-done.4
  45.6 25.0 %middle.1 = (bf16[1024,256]{1,0:T(8,128)(2,1)S(1)}, bf16[2048,256]{1,0:T(8,128)(2,1)S(1)}, bf16[256,2048]{1,0:T(8,128)(2,1)S(1)}, bf16[256,1024]{1,0:T(8,128)(2,...) custom-call(s32[8,128]{1,0:T(8,128)S(1)} %get-tuple-element.32.note_ref, ...), custom_call_target="tpu_custom_call" | custom-call | tf_op jit(solution)/shard_map/middle/pallas_call | solution.py:422
  70.6 32.0 %shifted_block.1 = bf16[1024,256]{1,0:T(8,128)(2,1)} custom-call(s32[16,128]{1,0:T(8,128)S(1)} %get-tuple-element.35.count_ref, f32[8,128]{1,0:T(8,128)S(1)} %get-tuple-element.36.peak_ref, bf16[2048,256]{1,0:T(8,128)(2,1)S(1)} %get-tuple-element.37.k_ref, bf16[256,2048]{1,0:T(8,128)(2,1)S(1)} %get-tuple-element.38.v_ref, ...), custom_call_target="tpu_custom_call" | custom-call | tf_op jit(solution)/shard_map/shifted_block/pallas_call | solution.py:468
Async XLA Ops:
  0.0 45.6 %copy-start.2 = (bf16[2,256,768]{2,1,0:T(8,128)(2,1)S(1)}, bf16[2,256,768]{2,1,0:T(8,128)(2,1)}, u32[]{:S(2)}) copy-start(bf16[2,256,768]{2,1,0:T(8,128)(2,1)} %qkv_ref.1) | copy-start | bytes 2359300
  18.9 26.7 %copy-start = (bf16[2,256,1024]{2,1,0:T(8,128)(2,1)S(1)}, bf16[2,256,1024]{2,1,0:T(8,128)(2,1)}, u32[]{:S(2)}) copy-start(bf16[2,256,1024]{2,1,0:T(8,128)(2,1)} %up_ref.3) | copy-start | bytes 3145732
  18.9 26.7 %copy-start.1 = (bf16[2,1024,256]{2,1,0:T(8,128)(2,1)S(1)}, bf16[2,1024,256]{2,1,0:T(8,128)(2,1)}, u32[]{:S(2)}) copy-start(bf16[2,1024,256]{2,1,0:T(8,128)(2,1)} %down_ref.3) | copy-start | bytes 3145732
  18.9 26.7 %copy-start.3 = (bf16[2,256,256]{2,1,0:T(8,128)(2,1)S(1)}, bf16[2,256,256]{2,1,0:T(8,128)(2,1)}, u32[]{:S(2)}) copy-start(bf16[2,256,256]{2,1,0:T(8,128)(2,1)} %out_ref.3) | copy-start | bytes 786436
  18.9 26.7 %copy-start.4 = (f32[2,4,256]{2,1,0:T(4,128)S(1)}, f32[2,4,256]{2,1,0:T(4,128)}, u32[]{:S(2)}) copy-start(f32[2,4,256]{2,1,0:T(4,128)} %norm_ref.3) | copy-start | bytes 24580

commit v3 on v2

--- a/solution.py
+++ b/solution.py
@@ -23,9 +23,10 @@
 SCORE_SCALE = HD**-0.5 * math.log2(math.e)
 SAFE_EXPONENT = 60.0
 SAFE_VALUE = 2.0**40
-UNROLL = 4
 EARLY = ((0, HALF, 0, HALF, False, False),)
-LATE = ((0, HALF, HALF, HALF, True, True), (HALF, HALF, 0, ROWS, False, True))
+LATER = ((0, HALF, HALF, STEP, True, False),)
+LAST = ((0, HALF, HALF + STEP, STEP, True, True),)
+OTHERS = ((HALF, HALF, 0, ROWS, False, True),)
 ALIGNED = ((0, HALF, 0, ROWS, False, True), (HALF, HALF, 0, ROWS, False, True))
 OWN = ((0, HALF, HALF, HALF, False, False), (HALF, HALF, ROWS, HALF, False, False))
 BORROWED = ((0, HALF, 0, HALF, True, True), (HALF, HALF, ROWS + HALF, HALF, True, True))
@@ -60,6 +61,19 @@
 
 def lane_valid(count):
     return jnp.where(lax.broadcasted_iota(I32, (1, CELL), 1) < count, 1.0, 0.0)
+
+
+def raise_peak(peak_ref, row, tall):
+    peak = peak_ref[row : row + 1, :]
+    for at in range(0, tall.shape[1], CELL):
+        peak = jnp.maximum(peak, tall[:, at : at + CELL])
+    peak_ref[row : row + 1, :] = peak
+
+
+def cells_in(rows, counts):
+    wide = rows.astype(F32)
+    cells = [first_valid(wide[u * CELL : (u + 1) * CELL], count) for u, count in enumerate(counts)]
+    return jnp.concatenate(cells, axis=0), jnp.concatenate([lane_valid(count) for count in counts], axis=1)
 
 
 def project(rows, valid, gain, offset, w_t, w_k, k_ref, v_ref, q_ref, peak_ref, k_at, q_at):
@@ -71,16 +85,14 @@
     v_ref[:, pl.ds(k_at, count)] = values.astype(BF16)
     wide = keys.astype(F32)
     sums = nn_dot((wide * wide).astype(BF16), head_pick(C, CELL, 0))
-    peak_ref[0:1, :] = jnp.maximum(peak_ref[0:1, :], jnp.max(sums, axis=0, keepdims=True))
-    tall = jnp.max(jnp.abs(values), axis=0, keepdims=True)
-    peak_ref[2:3, :] = jnp.maximum(peak_ref[2:3, :], jnp.maximum(tall[:, :CELL], tall[:, count - CELL :]))
+    raise_peak(peak_ref, 0, jnp.max(sums, axis=0, keepdims=True))
+    raise_peak(peak_ref, 2, jnp.max(jnp.abs(values), axis=0, keepdims=True))
     if q_at is not None:
         queries = nt_dot(w_t[:C, :], normed).astype(BF16)
         q_ref[:, pl.ds(q_at, count)] = queries
         wide = queries.astype(F32)
         sums = nn_dot(head_pick(HEADS, C, 1), (wide * wide).astype(BF16))
-        tall = jnp.max(sums, axis=0, keepdims=True)
-        peak_ref[1:2, :] = jnp.maximum(peak_ref[1:2, :], jnp.maximum(tall[:, :CELL], tall[:, count - CELL :]))
+        raise_peak(peak_ref, 1, jnp.max(sums, axis=0, keepdims=True))
 
 
 def turn(qkv_ref, w_ref):
@@ -88,52 +100,59 @@
         w_ref[at : at + C, :] = qkv_ref[:, source : source + C].astype(F32).T.astype(BF16)
 
 
-def attend(windows, pads, k_ref, v_ref, q_ref, m_ref, part, exact, unroll):
-    def one_head(head):
-        row = pl.ds(pl.multiple_of(head * HD, HD), HD)
-        half = pl.ds(pl.multiple_of((head // 8) * CELL, CELL), CELL)
+def attend(windows, pads, k_ref, v_ref, q_ref, m_ref, part, exact, unroll, group):
+    def some_heads(first):
+        rows = pl.ds(pl.multiple_of(first * HD, HD * group), HD * group)
+        half = pl.ds(pl.multiple_of((first // 8) * CELL, CELL), CELL)
         for q_lo, q_n, k_lo, k_n, goes_on, ends in windows:
             q_at = pl.ds(q_lo, q_n)
             lane_head = lax.broadcasted_iota(I32, (CELL, q_n), 0) // HD
             queries = q_ref[half, q_at]
-            queries = jnp.where(lane_head == head % 8, queries, jnp.zeros_like(queries))
+            queries = jnp.concatenate(
+                [jnp.where(lane_head == (first + g) % 8, queries, jnp.zeros_like(queries)) for g in range(group)],
+                axis=1)
             scores = nn_dot(k_ref[k_lo : k_lo + k_n, half], queries)
             if exact:
                 scores = scores - jnp.max(scores, axis=0, keepdims=True)
             weights = jnp.exp2(scores * SCORE_SCALE)
-            total = jnp.sum(jnp.sum(weights.reshape(k_n // 8, 8, q_n), axis=0), axis=0, keepdims=True)
+            totals = jnp.sum(jnp.sum(weights.reshape(k_n // 8, 8, group * q_n), axis=0), axis=0, keepdims=True)
             for cell in range(k_n // CELL):
-                total = total - pads[k_lo // CELL + cell] * weights[cell * CELL : cell * CELL + 1, :]
-            mixed = nn_dot(v_ref[row, k_lo : k_lo + k_n], weights.astype(BF16))
-            if goes_on:
-                mixed = mixed + part[0][row, q_at]
-                total = total + part[1][pl.ds(head, 1), q_at]
-            if ends:
-                m_ref[row, q_at] = (mixed / total).astype(BF16)
-            else:
-                part[0][row, q_at] = mixed
-                part[1][pl.ds(head, 1), q_at] = total
+                totals = totals - pads[k_lo // CELL + cell] * weights[cell * CELL : cell * CELL + 1, :]
+            mixes = nn_dot(v_ref[rows, k_lo : k_lo + k_n], weights.astype(BF16))
+            for g in range(group):
+                row = pl.ds(pl.multiple_of((first + g) * HD, HD), HD)
+                mixed = mixes[g * HD : (g + 1) * HD, g * q_n : (g + 1) * q_n]
+                total = totals[:, g * q_n : (g + 1) * q_n]
+                if goes_on:
+                    mixed = mixed + part[0][row, q_at]
+                    total = total + part[1][pl.ds(first + g, 1), q_at]
+                if ends:
+                    m_ref[row, q_at] = (mixed / total).astype(BF16)
+                else:
+                    part[0][row, q_at] = mixed
+                    part[1][pl.ds(first + g, 1), q_at] = total
 
     def step(i, carry):
         for u in range(unroll):
-            one_head(i * unroll + u)
+            some_heads((i * unroll + u) * group)
         return carry
 
-    lax.fori_loop(0, HEADS // unroll, step, 0)
-
-
-def attend_any(windows, whole_windows, pads, peak_ref, k_ref, v_ref, q_ref, m_ref, part):
+    lax.fori_loop(0, HEADS // (unroll * group), step, 0)
+
+
+def attend_any(plan, whole_windows, pads, peak_ref, k_ref, v_ref, q_ref, m_ref, part):
     bound = peak_ref[0:1, :] * peak_ref[1:2, :] * SCORE_SCALE**2
     off = (bound >= SAFE_EXPONENT * SAFE_EXPONENT) | (peak_ref[2:3, :] >= SAFE_VALUE)
     safe = jnp.max(jnp.where(off, 1.0, 0.0)) < 0.5
 
     @pl.when(safe)
     def _():
-        attend(windows, pads, k_ref, v_ref, q_ref, m_ref, part, False, UNROLL)
+        for windows, unroll, group in plan:
+            attend(windows, pads, k_ref, v_ref, q_ref, m_ref, part, False, unroll, group)
 
     @pl.when(jnp.logical_not(safe))
     def _():
-        attend(whole_windows, pads, k_ref, v_ref, q_ref, m_ref, part, True, 1)
+        attend(whole_windows, pads, k_ref, v_ref, q_ref, m_ref, part, True, 1, 1)
 
 
 def gelu(values):
@@ -177,10 +196,11 @@
         (norm_hbm, norm_ref, load_sem.at[2]), (qkv_hbm.at[0], qkv_ref, load_sem.at[3]),
     )
 
+    hops = (0, 0, 1, 3, 1, 3, 2, 2)
+    flips = (0, 1, 0, 0, 1, 1, 0, 1)
+
     def partner(i):
-        hop = i // 2
-        hop = 3 if hop == 2 else 2 if hop == 3 else hop
-        return lax.rem(me // 2 + hop, CELLS // 2) * 2 + lax.rem(me + i, 2)
+        return lax.rem(me // 2 + hops[i], CELLS // 2) * 2 + lax.rem(me + flips[i], 2)
 
     barrier = pltpu.get_barrier_semaphore()
     for i in range(1, CELLS):
@@ -212,7 +232,7 @@
         )
 
     copies = [sent(i) for i in range(1, CELLS)]
-    for pair in copies[:5]:
+    for pair in copies:
         for copy in pair:
             copy.start()
     finished(loads[2:])
@@ -220,44 +240,37 @@
     gain, offset = norm_ref[0, 0:1, :], norm_ref[0, 1:2, :]
     peak_ref[...] = jnp.zeros_like(peak_ref)
 
-    def take(j):
-        at = pl.multiple_of(j * CELL, CELL)
-        count = note_in[j, 1:2, :]
-        rows = first_valid(cells_ref[j].astype(F32), count[:, 0:1])
+    def take(i):
+        for pair in copies[max(i - 1, 0) : i + 1]:
+            for copy in pair:
+                copy.wait_recv()
+        rows, valid = cells_in(
+            jnp.concatenate([cells_ref[i], cells_ref[i + 1]], axis=0),
+            [note_in[i, 1:2, 0:1], note_in[i + 1, 1:2, 0:1]])
         project(
-            rows, lane_valid(count), gain, offset, w_ref[...], qkv_ref[:, C : 2 * C],
-            k_ref, v_ref, q_ref, peak_ref, at, at,
+            rows, valid, gain, offset, w_ref[...], qkv_ref[:, C : 2 * C],
+            k_ref, v_ref, q_ref, peak_ref, i * CELL, i * CELL,
         )
+
+    def pads(cells):
+        return [(CELL - note_in[i, 1:2, 0:1]).astype(F32) for i in range(cells)]
 
     cells_ref[0] = out_buf[me]
     note_in[0] = note_out[me]
+    part = (mixed_ref, total_ref)
     take(0)
-
-    def arrive(i):
-        for copy in copies[i - 1]:
-            copy.wait_recv()
-        take(i)
-
-    arrive(1)
-    for pair in copies[:5]:
-        for copy in pair:
-            copy.wait_send()
-    for pair in copies[5:]:
-        for copy in pair:
-            copy.start()
-    arrive(2)
-    arrive(3)
-    pads = [(CELL - note_in[j, 1:2, 0:1]).astype(F32) for j in range(CELLS // 2)]
-    attend(EARLY, pads, k_ref, v_ref, q_ref, None, (mixed_ref, total_ref), False, UNROLL)
-    for i in range(4, CELLS):
-        arrive(i)
+    take(2)
+    attend(EARLY, pads(4), k_ref, v_ref, q_ref, None, part, False, 1, 8)
+    take(4)
+    attend(LATER, pads(6), k_ref, v_ref, q_ref, None, part, False, 1, 8)
+    take(6)
     lane = lax.broadcasted_iota(I32, (CELLS, CELL), 1)
     meta = jnp.zeros((CELLS, CELL), I32)
     for j in range(CELLS):
         meta = jnp.where(lane == j, note_in[j], meta)
     meta_ref[...] = meta
     widest(peak_ref)
-    for pair in copies[5:]:
+    for pair in copies:
         for copy in pair:
             copy.wait_send()
 
@@ -311,7 +324,7 @@
 ):
     loads = started((meta_ref, place_ref, sem.at[0]))
     pads = [(CELL - meta_ref[1:2, j : j + 1]).astype(F32) for j in range(CELLS)]
-    attend_any(LATE, ALIGNED, pads, peak_ref, k_ref, v_ref, q_ref, mix_ref, (mixed_ref, total_ref))
+    attend_any(((LAST, 1, 8), (OTHERS, 8, 1)), ALIGNED, pads, peak_ref, k_ref, v_ref, q_ref, mix_ref, (mixed_ref, total_ref))
     finished(loads)
     for j in range(CELLS):
         to = place_ref[0, j]
@@ -372,43 +385,41 @@
             y_ref.at[pl.ds(HALF + i * STEP, STEP)], before_ref.at[pl.ds(i * STEP, STEP)],
             send_after.at[i], recv_before.at[i], device_id=after, device_id_type=MESH)
 
-    def place(rows, pair, k_at, q_at):
-        wide = rows.astype(F32)
-        wide = jnp.concatenate(
-            [first_valid(wide[u * CELL : (u + 1) * CELL], pair[u]) for u in range(2)], axis=0)
-        valid = jnp.concatenate([lane_valid(pair[u]) for u in range(2)], axis=1)
+    def place(rows, counts, k_at, q_at):
+        rows, valid = cells_in(rows, counts)
         project(
-            wide, valid, gain, offset, w_ref[...], qkv_ref[1, :, C : 2 * C],
+            rows, valid, gain, offset, w_ref[...], qkv_ref[1, :, C : 2 * C],
             k_ref, v_ref, q_ref, peak_ref, k_at, q_at,
         )
 
-    for i in range(2):
-        for chunk, copy in ((i, to_before(i)), (2 + i, to_after(i))):
-            at = chunk * STEP
-            cells = (2 * chunk, 2 * chunk + 1)
-            done = finish(
-                jnp.concatenate([x_ref[p] for p in cells], axis=0), m_ref[:, at : at + STEP],
-                norm_ref[0, 2:3, :], norm_ref[0, 3:4, :], out_ref[0], up_ref[0], down_ref[0],
-            )
-            y_ref[at : at + STEP, :] = done
-            place(done, [note_ref[p : p + 1, 0:1] for p in cells], HALF + at, at)
-            if i == 0 and chunk == 0:
-                pl.semaphore_wait(barrier, 2)
-                for note in notes:
-                    note.start()
-            copy.start()
-    pads = [None] * 4 + [(CELL - note_ref[p : p + 1, 0:1]).astype(F32) for p in range(CELLS)]
-    attend(OWN, pads, k_ref, v_ref, q_ref, None, (mixed_ref, total_ref), False, UNROLL)
+    pending = []
+    for chunk, copy in ((0, to_before(0)), (2, to_after(0)), (1, to_before(1)), (3, to_after(1))):
+        at = chunk * STEP
+        y_ref[at : at + STEP, :] = finish(
+            jnp.concatenate([x_ref[2 * chunk], x_ref[2 * chunk + 1]], axis=0), m_ref[:, at : at + STEP],
+            norm_ref[0, 2:3, :], norm_ref[0, 3:4, :], out_ref[0], up_ref[0], down_ref[0],
+        )
+        if not pending:
+            pl.semaphore_wait(barrier, 2)
+            for note in notes:
+                note.start()
+        else:
+            pending[-1].start()
+        pending.append(copy)
+    own = [note_ref[p : p + 1, 0:1] for p in range(CELLS)]
+    place(y_ref[:HALF, :], own[:4], HALF, 0)
+    pending[-1].start()
+    place(y_ref[HALF:, :], own[4:], ROWS, HALF)
+    pads = [None] * 4 + [(CELL - count).astype(F32) for count in own]
+    attend(OWN, pads, k_ref, v_ref, q_ref, None, (mixed_ref, total_ref), False, 1, 8)
     for copy in notes:
         copy.wait()
-    for i in range(2):
-        for incoming, source, note, first, k_first in (
-            (to_before(i), after_ref, note_after, 2 * i, HALF + ROWS),
-            (to_after(i), before_ref, note_before, CELLS // 2 + 2 * i, 0),
-        ):
-            incoming.wait_recv()
-            pair = [note[first + u : first + u + 1, 0:1] for u in range(2)]
-            place(source[i * STEP : (i + 1) * STEP, :], pair, k_first + i * STEP, None)
+    for incoming, source, note, first, k_first in (
+        (to_before, after_ref, note_after, 0, HALF + ROWS), (to_after, before_ref, note_before, 4, 0),
+    ):
+        for i in range(2):
+            incoming(i).wait_recv()
+        place(source[...], [note[first + u : first + u + 1, 0:1] for u in range(4)], k_first, None)
     all_count_ref[0:4, :] = note_before[4:8, :]
     all_count_ref[4:12, :] = note_ref[...]
     all_count_ref[12:16, :] = note_after[0:4, :]
@@ -446,20 +457,20 @@
     y_hbm, m_ref, y_ref, store_sem,
 ):
     pads = [(CELL - count_ref[j : j + 1, 0:1]).astype(F32) for j in range(2 * CELLS)]
-    attend_any(BORROWED, SHIFTED, pads, peak_ref, k_ref, v_ref, q_ref, m_ref, (mixed_ref, total_ref))
+    attend_any(((BORROWED, 2, 4),), SHIFTED, pads, peak_ref, k_ref, v_ref, q_ref, m_ref, (mixed_ref, total_ref))
     stores = []
-    for i in range(ROWS // STEP):
-        at = i * STEP
+    for i in range(ROWS // HALF):
+        at = i * HALF
         done = finish(
-            x_ref[at : at + STEP, :], m_ref[:, at : at + STEP], norm_ref[1, 2:3, :], norm_ref[1, 3:4, :],
+            x_ref[at : at + HALF, :], m_ref[:, at : at + HALF], norm_ref[1, 2:3, :], norm_ref[1, 3:4, :],
             out_ref[1], up_ref[1], down_ref[1],
         )
-        for u in range(2):
-            cell = CELLS // 2 + 2 * i + u
+        for u in range(4):
+            cell = CELLS // 2 + 4 * i + u
             keep = lax.broadcasted_iota(I32, (CELL, 1), 0) < count_ref[cell : cell + 1, 0:1]
             part = done[u * CELL : (u + 1) * CELL, :]
             y_ref[at + u * CELL : at + (u + 1) * CELL, :] = jnp.where(keep, part, jnp.zeros_like(part))
-        rows = pl.ds(at, STEP)
+        rows = pl.ds(at, HALF)
         stores += started((y_ref.at[rows], y_hbm.at[rows], store_sem.at[i]))
     finished(stores)
 

time: 103 us -> 98.1 us (0.952)
  Pallas kernels: 102 us -> 97.7 us
    pallas_call x1, Pallas kernels: 18.9 us -> 16.5 us  [gather_cells(): pl.pallas_call(gather_kernel, out_shape=(shape((CELLS, CELL, C)), shape((...]
    pallas_call x1, Pallas kernels: 25 us -> 22.7 us  [middle(): pl.pallas_call(middle_kernel, out_shape=(shape((ROWS, C)), shape((2 * ROW...]
where the time goes in v3:
time: 98.1 us; the launch traced here: 98 us
  Pallas kernels  97.7 us (100%)
    pallas_call x1, Pallas kernels, shifted_block(): pl.pallas_call(shifted_kernel, out_shape=shape((ROWS, C)), in_specs=[vmem...  31.8 us
    pallas_call x1, Pallas kernels, aligned_attention(): pl.pallas_call(aligned_kernel, out_shape=(shape((C, ROWS)), shape((CELLS,...  26.7 us
    pallas_call x1, Pallas kernels, middle(): pl.pallas_call(middle_kernel, out_shape=(shape((ROWS, C)), shape((2 * ROW...  22.7 us
    pallas_call x1, Pallas kernels, gather_cells(): pl.pallas_call(gather_kernel, out_shape=(shape((CELLS, CELL, C)), shape((...  16.5 us

profile of v3, /device:TPU:1, one launch (start us, length us, event | category | flops | bytes accessed | tf_op | source)
XLA Modules:
  0.0 98.0 jit_solution(430519500996045074)
XLA Ops:
  0.0 0.0 copy-start.2
  0.0 16.5 %gather_cells.1 = (bf16[8,128,256]{2,1,0:T(8,128)(2,1)S(1)}, bf16[1024,256]{1,0:T(8,128)(2,1)S(1)}, bf16[256,1024]{1,0:T(8,128)(2,1)S(1)}, bf16[256,1024]{1,0:T(...) custom-call(s32[8]{0:T(128)} %pos_hbm.1, ...), custom_call_target="tpu_custom_call" | custom-call | tf_op jit(solution)/shard_map/gather_cells/pallas_call | solution.py:295
  16.5 0.0 copy-start
  16.5 0.0 copy-start.1
  16.6 0.0 copy-start.3
  16.6 0.0 copy-start.4
  16.6 26.7 %aligned_attention.1 = (bf16[256,1024]{1,0:T(8,128)(2,1)S(1)}, bf16[8,128,256]{2,1,0:T(8,128)(2,1)S(1)}, s32[8,128]{1,0:T(8,128)S(1)}) custom-call(s32[8,128]{1,0:T(8,128)S(1)} %get-tuple-element.24.meta_ref, f32[8,128]{1,0:T(8,128)S(1)} %get-tuple-element.25.peak_ref, bf16[1024,256]{1,0:T(8,128)(2,1)S(1)} %get-tuple-element.26.k_ref, ...), custom_call_target="tpu_custom_call" | custom-call | tf_op jit(solution)/shard_map/aligned_attention/pallas_call | solution.py:337
  43.3 0.0 copy-done.2
  43.3 0.0 copy-done
  43.3 0.0 copy-done.1
  43.3 0.0 copy-done.3
  43.3 0.0 copy-done.4
  43.3 22.7 %middle.1 = (bf16[1024,256]{1,0:T(8,128)(2,1)S(1)}, bf16[2048,256]{1,0:T(8,128)(2,1)S(1)}, bf16[256,2048]{1,0:T(8,128)(2,1)S(1)}, bf16[256,1024]{1,0:T(8,128)(2,...) custom-call(s32[8,128]{1,0:T(8,128)S(1)} %get-tuple-element.32.note_ref, ...), custom_call_target="tpu_custom_call" | custom-call | tf_op jit(solution)/shard_map/middle/pallas_call | solution.py:433
  66.0 31.8 %shifted_block.1 = bf16[1024,256]{1,0:T(8,128)(2,1)} custom-call(s32[16,128]{1,0:T(8,128)S(1)} %get-tuple-element.35.count_ref, f32[8,128]{1,0:T(8,128)S(1)} %get-tuple-element.36.peak_ref, bf16[2048,256]{1,0:T(8,128)(2,1)S(1)} %get-tuple-element.37.k_ref, bf16[256,2048]{1,0:T(8,128)(2,1)S(1)} %get-tuple-element.38.v_ref, ...), custom_call_target="tpu_custom_call" | custom-call | tf_op jit(solution)/shard_map/shifted_block/pallas_call | solution.py:479
Async XLA Ops:
  0.0 43.3 %copy-start.2 = (bf16[2,256,768]{2,1,0:T(8,128)(2,1)S(1)}, bf16[2,256,768]{2,1,0:T(8,128)(2,1)}, u32[]{:S(2)}) copy-start(bf16[2,256,768]{2,1,0:T(8,128)(2,1)} %qkv_ref.1) | copy-start | bytes 2359300
  16.5 26.8 %copy-start = (bf16[2,256,1024]{2,1,0:T(8,128)(2,1)S(1)}, bf16[2,256,1024]{2,1,0:T(8,128)(2,1)}, u32[]{:S(2)}) copy-start(bf16[2,256,1024]{2,1,0:T(8,128)(2,1)} %up_ref.3) | copy-start | bytes 3145732
  16.5 26.8 %copy-start.1 = (bf16[2,1024,256]{2,1,0:T(8,128)(2,1)S(1)}, bf16[2,1024,256]{2,1,0:T(8,128)(2,1)}, u32[]{:S(2)}) copy-start(bf16[2,1024,256]{2,1,0:T(8,128)(2,1)} %down_ref.3) | copy-start | bytes 3145732
  16.6 26.8 %copy-start.3 = (bf16[2,256,256]{2,1,0:T(8,128)(2,1)S(1)}, bf16[2,256,256]{2,1,0:T(8,128)(2,1)}, u32[]{:S(2)}) copy-start(bf16[2,256,256]{2,1,0:T(8,128)(2,1)} %out_ref.3) | copy-start | bytes 786436
  16.6 26.8 %copy-start.4 = (f32[2,4,256]{2,1,0:T(4,128)S(1)}, f32[2,4,256]{2,1,0:T(4,128)}, u32[]{:S(2)}) copy-start(f32[2,4,256]{2,1,0:T(4,128)} %norm_ref.3) | copy-start | bytes 24580

commit v4 on v3

--- a/solution.py
+++ b/solution.py
@@ -29,7 +29,9 @@
 OTHERS = ((HALF, HALF, 0, ROWS, False, True),)
 ALIGNED = ((0, HALF, 0, ROWS, False, True), (HALF, HALF, 0, ROWS, False, True))
 OWN = ((0, HALF, HALF, HALF, False, False), (HALF, HALF, ROWS, HALF, False, False))
-BORROWED = ((0, HALF, 0, HALF, True, True), (HALF, HALF, ROWS + HALF, HALF, True, True))
+AFTER = ((HALF, HALF, ROWS + HALF, HALF, True, False),)
+BEFORE = ((0, HALF, 0, STEP, True, False),)
+BORROWED = ((0, HALF, STEP, STEP, True, True),)
 SHIFTED = ((0, HALF, 0, ROWS, False, True), (HALF, HALF, ROWS, ROWS, False, True))
 
 
@@ -140,7 +142,7 @@
     lax.fori_loop(0, HEADS // (unroll * group), step, 0)
 
 
-def attend_any(plan, whole_windows, pads, peak_ref, k_ref, v_ref, q_ref, m_ref, part):
+def attend_any(plan, whole_windows, settled, pads, peak_ref, k_ref, v_ref, q_ref, m_ref, part):
     bound = peak_ref[0:1, :] * peak_ref[1:2, :] * SCORE_SCALE**2
     off = (bound >= SAFE_EXPONENT * SAFE_EXPONENT) | (peak_ref[2:3, :] >= SAFE_VALUE)
     safe = jnp.max(jnp.where(off, 1.0, 0.0)) < 0.5
@@ -149,6 +151,9 @@
     def _():
         for windows, unroll, group in plan:
             attend(windows, pads, k_ref, v_ref, q_ref, m_ref, part, False, unroll, group)
+        for head in range(HEADS if settled is not None else 0):
+            row = slice(head * HD, (head + 1) * HD)
+            m_ref[row, settled:] = (part[0][row, settled:] / part[1][head : head + 1, settled:]).astype(BF16)
 
     @pl.when(jnp.logical_not(safe))
     def _():
@@ -324,7 +329,7 @@
 ):
     loads = started((meta_ref, place_ref, sem.at[0]))
     pads = [(CELL - meta_ref[1:2, j : j + 1]).astype(F32) for j in range(CELLS)]
-    attend_any(((LAST, 1, 8), (OTHERS, 8, 1)), ALIGNED, pads, peak_ref, k_ref, v_ref, q_ref, mix_ref, (mixed_ref, total_ref))
+    attend_any(((LAST, 1, 8), (OTHERS, 8, 1)), ALIGNED, None, pads, peak_ref, k_ref, v_ref, q_ref, mix_ref, (mixed_ref, total_ref))
     finished(loads)
     for j in range(CELLS):
         to = place_ref[0, j]
@@ -392,34 +397,36 @@
             k_ref, v_ref, q_ref, peak_ref, k_at, q_at,
         )
 
-    pending = []
-    for chunk, copy in ((0, to_before(0)), (2, to_after(0)), (1, to_before(1)), (3, to_after(1))):
+    for chunk in (2, 3, 0, 1):
         at = chunk * STEP
         y_ref[at : at + STEP, :] = finish(
             jnp.concatenate([x_ref[2 * chunk], x_ref[2 * chunk + 1]], axis=0), m_ref[:, at : at + STEP],
             norm_ref[0, 2:3, :], norm_ref[0, 3:4, :], out_ref[0], up_ref[0], down_ref[0],
         )
-        if not pending:
-            pl.semaphore_wait(barrier, 2)
-            for note in notes:
-                note.start()
-        else:
-            pending[-1].start()
-        pending.append(copy)
+    pl.semaphore_wait(barrier, 2)
+    for copy in notes + [to_after(0), to_after(1), to_before(0)]:
+        copy.start()
     own = [note_ref[p : p + 1, 0:1] for p in range(CELLS)]
+    place(y_ref[HALF:, :], own[4:], ROWS, HALF)
+    to_before(1).start()
     place(y_ref[:HALF, :], own[:4], HALF, 0)
-    pending[-1].start()
-    place(y_ref[HALF:, :], own[4:], ROWS, HALF)
+    part = (mixed_ref, total_ref)
     pads = [None] * 4 + [(CELL - count).astype(F32) for count in own]
-    attend(OWN, pads, k_ref, v_ref, q_ref, None, (mixed_ref, total_ref), False, 1, 8)
+    attend(OWN, pads, k_ref, v_ref, q_ref, None, part, False, 1, 8)
     for copy in notes:
         copy.wait()
-    for incoming, source, note, first, k_first in (
-        (to_before, after_ref, note_after, 0, HALF + ROWS), (to_after, before_ref, note_before, 4, 0),
-    ):
-        for i in range(2):
-            incoming(i).wait_recv()
-        place(source[...], [note[first + u : first + u + 1, 0:1] for u in range(4)], k_first, None)
+    before_counts = [note_before[p : p + 1, 0:1] for p in range(4, 8)]
+    after_counts = [note_after[p : p + 1, 0:1] for p in range(4)]
+    pads = [(CELL - count).astype(F32) for count in before_counts + own + after_counts]
+    for i in range(2):
+        to_before(i).wait_recv()
+    place(after_ref[...], after_counts, HALF + ROWS, None)
+    attend(AFTER, pads, k_ref, v_ref, q_ref, None, part, False, 1, 8)
+    to_after(0).wait_recv()
+    place(before_ref[:STEP, :], before_counts[:2], 0, None)
+    attend(BEFORE, pads, k_ref, v_ref, q_ref, None, part, False, 1, 8)
+    to_after(1).wait_recv()
+    place(before_ref[STEP:, :], before_counts[2:], STEP, None)
     all_count_ref[0:4, :] = note_before[4:8, :]
     all_count_ref[4:12, :] = note_ref[...]
     all_count_ref[12:16, :] = note_after[0:4, :]
@@ -457,7 +464,7 @@
     y_hbm, m_ref, y_ref, store_sem,
 ):
     pads = [(CELL - count_ref[j : j + 1, 0:1]).astype(F32) for j in range(2 * CELLS)]
-    attend_any(((BORROWED, 2, 4),), SHIFTED, pads, peak_ref, k_ref, v_ref, q_ref, m_ref, (mixed_ref, total_ref))
+    attend_any(((BORROWED, 1, 8),), SHIFTED, HALF, pads, peak_ref, k_ref, v_ref, q_ref, m_ref, (mixed_ref, total_ref))
     stores = []
     for i in range(ROWS // HALF):
         at = i * HALF

time: 98.1 us -> 102 us (1.040)
  Pallas kernels: 97.7 us -> 101 us
    pallas_call x1, Pallas kernels: 22.7 us -> 26.1 us  [middle(): pl.pallas_call(middle_kernel, out_shape=(shape((ROWS, C)), shape((2 * ROW...]
where the time goes in v4:
time: 102 us; the launch traced here: 101 us
  Pallas kernels  101 us (99%)
    pallas_call x1, Pallas kernels, shifted_block(): pl.pallas_call(shifted_kernel, out_shape=shape((ROWS, C)), in_specs=[vmem...  31.8 us
    pallas_call x1, Pallas kernels, aligned_attention(): pl.pallas_call(aligned_kernel, out_shape=(shape((C, ROWS)), shape((CELLS,...  26.7 us
    pallas_call x1, Pallas kernels, middle(): pl.pallas_call(middle_kernel, out_shape=(shape((ROWS, C)), shape((2 * ROW...  26.1 us
    pallas_call x1, Pallas kernels, gather_cells(): pl.pallas_call(gather_kernel, out_shape=(shape((CELLS, CELL, C)), shape((...  16.5 us

profile of v4, /device:TPU:1, one launch (start us, length us, event | category | flops | bytes accessed | tf_op | source)
XLA Modules:
  0.0 101.4 jit_solution(15447342942731930670)
XLA Ops:
  0.0 0.0 copy-start.2
  0.0 16.5 %gather_cells.1 = (bf16[8,128,256]{2,1,0:T(8,128)(2,1)S(1)}, bf16[1024,256]{1,0:T(8,128)(2,1)S(1)}, bf16[256,1024]{1,0:T(8,128)(2,1)S(1)}, bf16[256,1024]{1,0:T(...) custom-call(s32[8]{0:T(128)} %pos_hbm.1, ...), custom_call_target="tpu_custom_call" | custom-call | tf_op jit(solution)/shard_map/gather_cells/pallas_call | solution.py:300
  16.5 0.0 copy-start
  16.5 0.0 copy-start.1
  16.6 0.0 copy-start.3
  16.6 0.0 copy-start.4
  16.6 26.7 %aligned_attention.1 = (bf16[256,1024]{1,0:T(8,128)(2,1)S(1)}, bf16[8,128,256]{2,1,0:T(8,128)(2,1)S(1)}, s32[8,128]{1,0:T(8,128)S(1)}) custom-call(s32[8,128]{1,0:T(8,128)S(1)} %get-tuple-element.24.meta_ref, f32[8,128]{1,0:T(8,128)S(1)} %get-tuple-element.25.peak_ref, bf16[1024,256]{1,0:T(8,128)(2,1)S(1)} %get-tuple-element.26.k_ref, ...), custom_call_target="tpu_custom_call" | custom-call | tf_op jit(solution)/shard_map/aligned_attention/pallas_call | solution.py:342
  43.3 0.0 copy-done.2
  43.3 0.0 copy-done
  43.3 0.0 copy-done.1
  43.3 0.0 copy-done.3
  43.3 0.0 copy-done.4
  43.3 26.1 %middle.1 = (bf16[1024,256]{1,0:T(8,128)(2,1)S(1)}, bf16[2048,256]{1,0:T(8,128)(2,1)S(1)}, bf16[256,2048]{1,0:T(8,128)(2,1)S(1)}, bf16[256,1024]{1,0:T(8,128)(2,...) custom-call(s32[8,128]{1,0:T(8,128)S(1)} %get-tuple-element.32.note_ref, ...), custom_call_target="tpu_custom_call" | custom-call | tf_op jit(solution)/shard_map/middle/pallas_call | solution.py:440
  69.4 31.8 %shifted_block.1 = bf16[1024,256]{1,0:T(8,128)(2,1)} custom-call(s32[16,128]{1,0:T(8,128)S(1)} %get-tuple-element.35.count_ref, f32[8,128]{1,0:T(8,128)S(1)} %get-tuple-element.36.peak_ref, bf16[2048,256]{1,0:T(8,128)(2,1)S(1)} %get-tuple-element.37.k_ref, bf16[256,2048]{1,0:T(8,128)(2,1)S(1)} %get-tuple-element.38.v_ref, ...), custom_call_target="tpu_custom_call" | custom-call | tf_op jit(solution)/shard_map/shifted_block/pallas_call | solution.py:486
Async XLA Ops:
  0.0 43.3 %copy-start.2 = (bf16[2,256,768]{2,1,0:T(8,128)(2,1)S(1)}, bf16[2,256,768]{2,1,0:T(8,128)(2,1)}, u32[]{:S(2)}) copy-start(bf16[2,256,768]{2,1,0:T(8,128)(2,1)} %qkv_ref.1) | copy-start | bytes 2359300
  16.5 26.8 %copy-start = (bf16[2,256,1024]{2,1,0:T(8,128)(2,1)S(1)}, bf16[2,256,1024]{2,1,0:T(8,128)(2,1)}, u32[]{:S(2)}) copy-start(bf16[2,256,1024]{2,1,0:T(8,128)(2,1)} %up_ref.3) | copy-start | bytes 3145732
  16.5 26.8 %copy-start.1 = (bf16[2,1024,256]{2,1,0:T(8,128)(2,1)S(1)}, bf16[2,1024,256]{2,1,0:T(8,128)(2,1)}, u32[]{:S(2)}) copy-start(bf16[2,1024,256]{2,1,0:T(8,128)(2,1)} %down_ref.3) | copy-start | bytes 3145732
  16.6 26.8 %copy-start.3 = (bf16[2,256,256]{2,1,0:T(8,128)(2,1)S(1)}, bf16[2,256,256]{2,1,0:T(8,128)(2,1)}, u32[]{:S(2)}) copy-start(bf16[2,256,256]{2,1,0:T(8,128)(2,1)} %out_ref.3) | copy-start | bytes 786436
  16.6 26.8 %copy-start.4 = (f32[2,4,256]{2,1,0:T(4,128)S(1)}, f32[2,4,256]{2,1,0:T(4,128)}, u32[]{:S(2)}) copy-start(f32[2,4,256]{2,1,0:T(4,128)} %norm_ref.3) | copy-start | bytes 24580

commit v5 on v4

--- a/solution.py
+++ b/solution.py
@@ -364,13 +364,12 @@
 def middle_kernel(
     note_ref, x_ref, m_ref, norm_ref, qkv_ref, out_ref, up_ref, down_ref,
     y_ref, k_ref, v_ref, q_ref, all_count_ref, peak_ref, mixed_ref, total_ref,
-    before_ref, after_ref, note_before, note_after, w_ref,
+    before_ref, after_ref, note_before, note_after, w_ref, ready,
     send_before, send_after, recv_before, recv_after, note_send, note_recv,
 ):
     after, before = along(1), along(-1)
     barrier = pltpu.get_barrier_semaphore()
-    for device in (after, before):
-        pl.semaphore_signal(barrier, inc=1, device_id=device, device_id_type=MESH)
+    pl.semaphore_signal(barrier, inc=1, device_id=before, device_id_type=MESH)
     turn(qkv_ref.at[1], w_ref)
     gain, offset = norm_ref[1, 0:1, :], norm_ref[1, 1:2, :]
     peak_ref[...] = jnp.zeros_like(peak_ref)
@@ -403,13 +402,18 @@
             jnp.concatenate([x_ref[2 * chunk], x_ref[2 * chunk + 1]], axis=0), m_ref[:, at : at + STEP],
             norm_ref[0, 2:3, :], norm_ref[0, 3:4, :], out_ref[0], up_ref[0], down_ref[0],
         )
-    pl.semaphore_wait(barrier, 2)
-    for copy in notes + [to_after(0), to_after(1), to_before(0)]:
-        copy.start()
+        if chunk == 3:
+            pl.semaphore_wait(barrier, 1)
+            pl.semaphore_signal(ready, inc=1, device_id=after, device_id_type=MESH)
+            notes[1].start()
+            to_after(0).start()
+    to_after(1).start()
     own = [note_ref[p : p + 1, 0:1] for p in range(CELLS)]
     place(y_ref[HALF:, :], own[4:], ROWS, HALF)
-    to_before(1).start()
     place(y_ref[:HALF, :], own[:4], HALF, 0)
+    pl.semaphore_wait(ready, 1)
+    for copy in (notes[0], to_before(0), to_before(1)):
+        copy.start()
     part = (mixed_ref, total_ref)
     pads = [None] * 4 + [(CELL - count).astype(F32) for count in own]
     attend(OWN, pads, k_ref, v_ref, q_ref, None, part, False, 1, 8)
@@ -451,6 +455,7 @@
             pltpu.VMEM((CELLS, CELL), I32),
             pltpu.VMEM((CELLS, CELL), I32),
             pltpu.VMEM((2 * C, C), BF16),
+            pltpu.SemaphoreType.REGULAR,
             dma(2), dma(2), dma(2), dma(2), dma(2), dma(2),
         ],
         compiler_params=pltpu.CompilerParams(

time: 102 us -> 101 us (level)
  no operation moved by 1% of the time
where the time goes in v5:
time: 101 us
  Pallas kernels  100 us (99%)
    pallas_call x1, Pallas kernels, shifted_block(): pl.pallas_call(shifted_kernel, out_shape=shape((ROWS, C)), in_specs=[vmem...  31.8 us
    pallas_call x1, Pallas kernels, aligned_attention(): pl.pallas_call(aligned_kernel, out_shape=(shape((C, ROWS)), shape((CELLS,...  26.7 us
    pallas_call x1, Pallas kernels, middle(): pl.pallas_call(middle_kernel, out_shape=(shape((ROWS, C)), shape((2 * ROW...  25.4 us
    pallas_call x1, Pallas kernels, gather_cells(): pl.pallas_call(gather_kernel, out_shape=(shape((CELLS, CELL, C)), shape((...  16.5 us

profile of v5, /device:TPU:1, one launch (start us, length us, event | category | flops | bytes accessed | tf_op | source)
XLA Modules:
  0.0 100.7 jit_solution(3953109326527682667)
XLA Ops:
  0.0 0.0 copy-start.2
  0.0 16.5 %gather_cells.1 = (bf16[8,128,256]{2,1,0:T(8,128)(2,1)S(1)}, bf16[1024,256]{1,0:T(8,128)(2,1)S(1)}, bf16[256,1024]{1,0:T(8,128)(2,1)S(1)}, bf16[256,1024]{1,0:T(...) custom-call(s32[8]{0:T(128)} %pos_hbm.1, ...), custom_call_target="tpu_custom_call" | custom-call | tf_op jit(solution)/shard_map/gather_cells/pallas_call | solution.py:300
  16.5 0.0 copy-start
  16.5 0.0 copy-start.1
  16.6 0.0 copy-start.3
  16.6 0.0 copy-start.4
  16.6 26.7 %aligned_attention.1 = (bf16[256,1024]{1,0:T(8,128)(2,1)S(1)}, bf16[8,128,256]{2,1,0:T(8,128)(2,1)S(1)}, s32[8,128]{1,0:T(8,128)S(1)}) custom-call(s32[8,128]{1,0:T(8,128)S(1)} %get-tuple-element.24.meta_ref, f32[8,128]{1,0:T(8,128)S(1)} %get-tuple-element.25.peak_ref, bf16[1024,256]{1,0:T(8,128)(2,1)S(1)} %get-tuple-element.26.k_ref, ...), custom_call_target="tpu_custom_call" | custom-call | tf_op jit(solution)/shard_map/aligned_attention/pallas_call | solution.py:342
  43.3 0.0 copy-done.2
  43.3 0.0 copy-done
  43.3 0.0 copy-done.1
  43.3 0.0 copy-done.3
  43.3 0.0 copy-done.4
  43.3 25.4 %middle.1 = (bf16[1024,256]{1,0:T(8,128)(2,1)S(1)}, bf16[2048,256]{1,0:T(8,128)(2,1)S(1)}, bf16[256,2048]{1,0:T(8,128)(2,1)S(1)}, bf16[256,1024]{1,0:T(8,128)(2,...) custom-call(s32[8,128]{1,0:T(8,128)S(1)} %get-tuple-element.32.note_ref, ...), custom_call_target="tpu_custom_call" | custom-call | tf_op jit(solution)/shard_map/middle/pallas_call | solution.py:444
  68.7 31.8 %shifted_block.1 = bf16[1024,256]{1,0:T(8,128)(2,1)} custom-call(s32[16,128]{1,0:T(8,128)S(1)} %get-tuple-element.35.count_ref, f32[8,128]{1,0:T(8,128)S(1)} %get-tuple-element.36.peak_ref, bf16[2048,256]{1,0:T(8,128)(2,1)S(1)} %get-tuple-element.37.k_ref, bf16[256,2048]{1,0:T(8,128)(2,1)S(1)} %get-tuple-element.38.v_ref, ...), custom_call_target="tpu_custom_call" | custom-call | tf_op jit(solution)/shard_map/shifted_block/pallas_call | solution.py:491
Async XLA Ops:
  0.0 43.3 %copy-start.2 = (bf16[2,256,768]{2,1,0:T(8,128)(2,1)S(1)}, bf16[2,256,768]{2,1,0:T(8,128)(2,1)}, u32[]{:S(2)}) copy-start(bf16[2,256,768]{2,1,0:T(8,128)(2,1)} %qkv_ref.1) | copy-start | bytes 2359300
  16.5 26.8 %copy-start = (bf16[2,256,1024]{2,1,0:T(8,128)(2,1)S(1)}, bf16[2,256,1024]{2,1,0:T(8,128)(2,1)}, u32[]{:S(2)}) copy-start(bf16[2,256,1024]{2,1,0:T(8,128)(2,1)} %up_ref.3) | copy-start | bytes 3145732
  16.5 26.8 %copy-start.1 = (bf16[2,1024,256]{2,1,0:T(8,128)(2,1)S(1)}, bf16[2,1024,256]{2,1,0:T(8,128)(2,1)}, u32[]{:S(2)}) copy-start(bf16[2,1024,256]{2,1,0:T(8,128)(2,1)} %down_ref.3) | copy-start | bytes 3145732
  16.6 26.8 %copy-start.3 = (bf16[2,256,256]{2,1,0:T(8,128)(2,1)S(1)}, bf16[2,256,256]{2,1,0:T(8,128)(2,1)}, u32[]{:S(2)}) copy-start(bf16[2,256,256]{2,1,0:T(8,128)(2,1)} %out_ref.3) | copy-start | bytes 786436
  16.6 26.8 %copy-start.4 = (f32[2,4,256]{2,1,0:T(4,128)S(1)}, f32[2,4,256]{2,1,0:T(4,128)}, u32[]{:S(2)}) copy-start(f32[2,4,256]{2,1,0:T(4,128)} %norm_ref.3) | copy-start | bytes 24580

commit v6 on v5

--- a/solution.py
+++ b/solution.py
@@ -102,7 +102,7 @@
         w_ref[at : at + C, :] = qkv_ref[:, source : source + C].astype(F32).T.astype(BF16)
 
 
-def attend(windows, pads, k_ref, v_ref, q_ref, m_ref, part, exact, unroll, group):
+def attend(windows, pads, k_ref, v_ref, q_ref, m_ref, part, exact, unroll, group, first=0, last=HEADS):
     def some_heads(first):
         rows = pl.ds(pl.multiple_of(first * HD, HD * group), HD * group)
         half = pl.ds(pl.multiple_of((first // 8) * CELL, CELL), CELL)
@@ -139,7 +139,7 @@
             some_heads((i * unroll + u) * group)
         return carry
 
-    lax.fori_loop(0, HEADS // (unroll * group), step, 0)
+    lax.fori_loop(first // (unroll * group), last // (unroll * group), step, 0)
 
 
 def attend_any(plan, whole_windows, settled, pads, peak_ref, k_ref, v_ref, q_ref, m_ref, part):
@@ -402,33 +402,36 @@
             jnp.concatenate([x_ref[2 * chunk], x_ref[2 * chunk + 1]], axis=0), m_ref[:, at : at + STEP],
             norm_ref[0, 2:3, :], norm_ref[0, 3:4, :], out_ref[0], up_ref[0], down_ref[0],
         )
-        if chunk == 3:
+        if chunk == 2:
             pl.semaphore_wait(barrier, 1)
             pl.semaphore_signal(ready, inc=1, device_id=after, device_id_type=MESH)
             notes[1].start()
+        if chunk == 3:
             to_after(0).start()
     to_after(1).start()
     own = [note_ref[p : p + 1, 0:1] for p in range(CELLS)]
     place(y_ref[HALF:, :], own[4:], ROWS, HALF)
     place(y_ref[:HALF, :], own[:4], HALF, 0)
+    part = (mixed_ref, total_ref)
+    pads = [None] * 4 + [(CELL - count).astype(F32) for count in own]
+    attend(OWN[:1], pads, k_ref, v_ref, q_ref, None, part, False, 1, 8, 0, 8)
     pl.semaphore_wait(ready, 1)
     for copy in (notes[0], to_before(0), to_before(1)):
         copy.start()
-    part = (mixed_ref, total_ref)
-    pads = [None] * 4 + [(CELL - count).astype(F32) for count in own]
-    attend(OWN, pads, k_ref, v_ref, q_ref, None, part, False, 1, 8)
+    attend(OWN[:1], pads, k_ref, v_ref, q_ref, None, part, False, 1, 8, 8, HEADS)
+    attend(OWN[1:], pads, k_ref, v_ref, q_ref, None, part, False, 1, 8)
     for copy in notes:
         copy.wait()
     before_counts = [note_before[p : p + 1, 0:1] for p in range(4, 8)]
     after_counts = [note_after[p : p + 1, 0:1] for p in range(4)]
     pads = [(CELL - count).astype(F32) for count in before_counts + own + after_counts]
+    to_after(0).wait_recv()
+    place(before_ref[:STEP, :], before_counts[:2], 0, None)
+    attend(BEFORE, pads, k_ref, v_ref, q_ref, None, part, False, 1, 8)
     for i in range(2):
         to_before(i).wait_recv()
     place(after_ref[...], after_counts, HALF + ROWS, None)
     attend(AFTER, pads, k_ref, v_ref, q_ref, None, part, False, 1, 8)
-    to_after(0).wait_recv()
-    place(before_ref[:STEP, :], before_counts[:2], 0, None)
-    attend(BEFORE, pads, k_ref, v_ref, q_ref, None, part, False, 1, 8)
     to_after(1).wait_recv()
     place(before_ref[STEP:, :], before_counts[2:], STEP, None)
     all_count_ref[0:4, :] = note_before[4:8, :]

time: 101 us -> 98.7 us (0.977)
  Pallas kernels: 100 us -> 98.3 us
    pallas_call x1, Pallas kernels: 25.4 us -> 23.5 us  [middle(): pl.pallas_call(middle_kernel, out_shape=(shape((ROWS, C)), shape((2 * ROW...]
where the time goes in v6:
time: 98.7 us; the launch traced here: 98.6 us
  Pallas kernels  98.3 us (100%)
    pallas_call x1, Pallas kernels, shifted_block(): pl.pallas_call(shifted_kernel, out_shape=shape((ROWS, C)), in_specs=[vmem...  31.6 us
    pallas_call x1, Pallas kernels, aligned_attention(): pl.pallas_call(aligned_kernel, out_shape=(shape((C, ROWS)), shape((CELLS,...  26.7 us
    pallas_call x1, Pallas kernels, middle(): pl.pallas_call(middle_kernel, out_shape=(shape((ROWS, C)), shape((2 * ROW...  23.5 us
    pallas_call x1, Pallas kernels, gather_cells(): pl.pallas_call(gather_kernel, out_shape=(shape((CELLS, CELL, C)), shape((...  16.5 us

profile of v6, /device:TPU:1, one launch (start us, length us, event | category | flops | bytes accessed | tf_op | source)
XLA Modules:
  0.0 98.6 jit_solution(10522778104493919748)
XLA Ops:
  0.0 0.0 copy-start.2
  0.0 16.5 %gather_cells.1 = (bf16[8,128,256]{2,1,0:T(8,128)(2,1)S(1)}, bf16[1024,256]{1,0:T(8,128)(2,1)S(1)}, bf16[256,1024]{1,0:T(8,128)(2,1)S(1)}, bf16[256,1024]{1,0:T(...) custom-call(s32[8]{0:T(128)} %pos_hbm.1, ...), custom_call_target="tpu_custom_call" | custom-call | tf_op jit(solution)/shard_map/gather_cells/pallas_call | solution.py:300
  16.5 0.0 copy-start
  16.5 0.0 copy-start.1
  16.6 0.0 copy-start.3
  16.6 0.0 copy-start.4
  16.6 26.7 %aligned_attention.1 = (bf16[256,1024]{1,0:T(8,128)(2,1)S(1)}, bf16[8,128,256]{2,1,0:T(8,128)(2,1)S(1)}, s32[8,128]{1,0:T(8,128)S(1)}) custom-call(s32[8,128]{1,0:T(8,128)S(1)} %get-tuple-element.24.meta_ref, f32[8,128]{1,0:T(8,128)S(1)} %get-tuple-element.25.peak_ref, bf16[1024,256]{1,0:T(8,128)(2,1)S(1)} %get-tuple-element.26.k_ref, ...), custom_call_target="tpu_custom_call" | custom-call | tf_op jit(solution)/shard_map/aligned_attention/pallas_call | solution.py:342
  43.3 0.0 copy-done.2
  43.3 0.0 copy-done
  43.3 0.0 copy-done.1
  43.3 0.0 copy-done.3
  43.3 0.0 copy-done.4
  43.3 23.5 %middle.1 = (bf16[1024,256]{1,0:T(8,128)(2,1)S(1)}, bf16[2048,256]{1,0:T(8,128)(2,1)S(1)}, bf16[256,2048]{1,0:T(8,128)(2,1)S(1)}, bf16[256,1024]{1,0:T(8,128)(2,...) custom-call(s32[8,128]{1,0:T(8,128)S(1)} %get-tuple-element.32.note_ref, ...), custom_call_target="tpu_custom_call" | custom-call | tf_op jit(solution)/shard_map/middle/pallas_call | solution.py:447
  66.8 31.6 %shifted_block.1 = bf16[1024,256]{1,0:T(8,128)(2,1)} custom-call(s32[16,128]{1,0:T(8,128)S(1)} %get-tuple-element.35.count_ref, f32[8,128]{1,0:T(8,128)S(1)} %get-tuple-element.36.peak_ref, bf16[2048,256]{1,0:T(8,128)(2,1)S(1)} %get-tuple-element.37.k_ref, bf16[256,2048]{1,0:T(8,128)(2,1)S(1)} %get-tuple-element.38.v_ref, ...), custom_call_target="tpu_custom_call" | custom-call | tf_op jit(solution)/shard_map/shifted_block/pallas_call | solution.py:494
Async XLA Ops:
  0.0 43.3 %copy-start.2 = (bf16[2,256,768]{2,1,0:T(8,128)(2,1)S(1)}, bf16[2,256,768]{2,1,0:T(8,128)(2,1)}, u32[]{:S(2)}) copy-start(bf16[2,256,768]{2,1,0:T(8,128)(2,1)} %qkv_ref.1) | copy-start | bytes 2359300
  16.5 26.8 %copy-start = (bf16[2,256,1024]{2,1,0:T(8,128)(2,1)S(1)}, bf16[2,256,1024]{2,1,0:T(8,128)(2,1)}, u32[]{:S(2)}) copy-start(bf16[2,256,1024]{2,1,0:T(8,128)(2,1)} %up_ref.3) | copy-start | bytes 3145732
  16.5 26.8 %copy-start.1 = (bf16[2,1024,256]{2,1,0:T(8,128)(2,1)S(1)}, bf16[2,1024,256]{2,1,0:T(8,128)(2,1)}, u32[]{:S(2)}) copy-start(bf16[2,1024,256]{2,1,0:T(8,128)(2,1)} %down_ref.3) | copy-start | bytes 3145732
  16.6 26.8 %copy-start.3 = (bf16[2,256,256]{2,1,0:T(8,128)(2,1)S(1)}, bf16[2,256,256]{2,1,0:T(8,128)(2,1)}, u32[]{:S(2)}) copy-start(bf16[2,256,256]{2,1,0:T(8,128)(2,1)} %out_ref.3) | copy-start | bytes 786436
  16.6 26.8 %copy-start.4 = (f32[2,4,256]{2,1,0:T(4,128)S(1)}, f32[2,4,256]{2,1,0:T(4,128)}, u32[]{:S(2)}) copy-start(f32[2,4,256]{2,1,0:T(4,128)} %norm_ref.3) | copy-start | bytes 24580
